TPU v7x, 128 devices: a whole 4x4x4 slice. The times are simulated.
128 devices in a mesh: row: 16 (over y, z), col: 8 (over x, core).
Axes of the slice: x: 4, y: 4, z: 4, core: 2. Of those that a mesh axis runs over, the one named last changes fastest.
Arguments:
- points: float32 [32768, 64], P(('col', 'row')), may hold values from -6 to 6
- feature_scale: float32 [64], replicated, may hold values from 0.1 to 0.5
- test_matrix: bfloat16 [32768, 256], P(('col', 'row')), may hold values from -6 to 6
- targets: float32 [32768], P(('col', 'row')), may hold values from -6 to 6
- ridge: float32 [1], replicated, may hold values from 0.5 to 2
Outputs:
- coefficients: float32 [32768], P(('col', 'row'))
- residual: float32 [32768], P(('col', 'row'))
- sketch: float32 [32768, 256], P(('col', 'row'))
All inputs are finite; a program needn't handle non-finite values.
Results may differ from a plain program's by a relative error of at most 0.012.
The roundings to bfloat16 on the way count: a program that leaves them out, or rounds other values in their place, can miss the bound.
Values may be sent and summed in bfloat16 or wider, within the bound.
No kernel may reach another device: no remote copies, remote signals or barrier semaphores. Data moves between devices by JAX's collectives and lax.ppermute only.
A program may use at most 128 MiB of HBM per device.

v0:
```python
import functools

import jax
import jax.numpy as jnp
from jax import lax
from jax.experimental import pallas as pl
from jax.experimental.pallas import tpu as pltpu
from jax.sharding import Mesh
from jax.sharding import PartitionSpec as P


ROW = ("row_0", "row_1")
COL = ("col_0", "col_1")
COL_ROW = ("col_0", "col_1", "row_0", "row_1")
LOG2E = 1.4426950408889634
MIB = 1024 * 1024
F32 = jnp.float32
BF16 = jnp.bfloat16
HIGH = lax.Precision.HIGHEST
KERN_SPACE = pltpu.VMEM
ORDER = (2, 1, 3, 0)
LATE = ((0, 1), (3, 1))
KLIMIT = 4
KLIMIT2 = 4


def call(body, outs, *args, scratch=(), limit=4):
    return pl.pallas_call(
        body,
        out_shape=outs,
        scratch_shapes=list(scratch),
        compiler_params=pltpu.CompilerParams(vmem_limit_bytes=limit * MIB),
    )(*args)


def shape(*dims, dtype=F32):
    return jax.ShapeDtypeStruct(dims, dtype)


def exchanged(pieces, axes):
    return lax.all_to_all(pieces, axes, 0, 0, tiled=True)


def split3(value):
    first = value.astype(BF16)
    rest = value - first.astype(F32)
    second = rest.astype(BF16)
    third = (rest - second.astype(F32)).astype(BF16)
    return first, second, third


def parts_body(points_ref, scale_ref, test_ref, out_ref, copies_ref):
    y = points_ref[...] * (scale_ref[...] * LOG2E**0.5)
    first = y.astype(BF16).astype(F32)
    second = (y - first).astype(BF16).astype(F32)
    parts = jnp.concatenate([first, second], axis=1).astype(BF16)
    out_ref[...] = parts
    for i in range(copies_ref.shape[0]):
        copies_ref[i, :, 0:128] = parts
        copies_ref[i, :, 128:384] = test_ref[...]


def norms_body(message_ref, norm_ref):
    lane = lax.broadcasted_iota(jnp.int32, (128, 128), 1)
    sub = lax.broadcasted_iota(jnp.int32, (128, 128), 0)
    twice = jnp.where((lane - sub) % 64 == 0, 1.0, 0.0).astype(BF16)
    points = jnp.dot(message_ref[:, 0:128], twice, preferred_element_type=F32)
    squares = -0.25 * (points * points)
    lane8, sub8 = lane[0:8], sub[0:8]
    for base in range(0, message_ref.shape[0], 128):
        packed = jnp.zeros((8, 128), F32)
        for at in range(0, 128, 8):
            total = jnp.sum(squares[base + at : base + at + 8], axis=1, keepdims=True)
            packed = packed + jnp.where(lane8 == sub8 + at, total, 0.0)
        norm_ref[:, base : base + 128] = eight(jnp.sum(packed, axis=0, keepdims=True))


def block_body(first_ref, second_ref, message_ref, norm_ref, kern_ref, own_ref, other_ref, *, chunk):
    parts = jnp.concatenate([first_ref[...], second_ref[...]], axis=0)
    turned = pltpu.roll(parts.astype(F32), 64, 1)
    points = parts.astype(F32) + turned
    left_norm = -0.25 * jnp.sum(points * points, axis=1, keepdims=True)
    left = jnp.concatenate([parts, turned.astype(BF16)], axis=1)
    total = None
    for start in range(0, message_ref.shape[0], chunk):
        span = slice(start, start + chunk)
        right = message_ref[span, 0:128]
        exponent = lax.dot_general(
            left,
            jnp.concatenate([right, right], axis=1),
            (((1,), (1,)), ((), ())),
            preferred_element_type=F32,
        )
        weights = jnp.exp2(exponent + left_norm + norm_ref[0:1, span])
        kern_ref[:, span] = weights
        part = jnp.dot(
            weights.astype(BF16), message_ref[span, 128:], preferred_element_type=F32
        )
        total = part if total is None else total + part
    half = total.shape[0] // 2
    own_ref[...] = total[:half]
    other_ref[...] = total[half:]


def kernel_block(first, second, message, norm):
    rows, columns, rank = first.shape[0], message.shape[0], message.shape[1] - 128
    return call(
        functools.partial(block_body, chunk=512),
        [KERN_SPACE((2 * rows, columns), F32), shape(rows, rank), shape(rows, rank)],
        first,
        second,
        message,
        norm,
        limit=KLIMIT,
    )


def core_body(
    near_ref, swapped_ref, one_ref, two_ref, three_ref, test_ref, targets_ref, ridge_ref, sketch_ref, copy_ref, out_ref
):
    sketch = near_ref[...] + swapped_ref[...] + one_ref[...] + two_ref[...] + three_ref[...]
    sketch_ref[...] = sketch
    copy_ref[...] = sketch
    shifted = ridge_ref[0, 0] * test_ref[...].astype(F32) + sketch
    core = lax.dot_general(
        shifted, sketch, (((0,), (0,)), ((), ())), precision=HIGH, preferred_element_type=F32
    )
    targets = jnp.broadcast_to(targets_ref[...], (8, 256))
    projected = jnp.dot(targets, sketch, precision=HIGH, preferred_element_type=F32)
    square = jnp.sum(targets[0:1] * targets[0:1], axis=1, keepdims=True)
    row = lax.broadcasted_iota(jnp.int32, (8, 128), 0)
    extra = jnp.where(row == 2, square, 0.0)
    extra = jnp.where(row == 1, projected[:, 128:256], extra)
    extra = jnp.where(row == 0, projected[:, 0:128], extra)
    out_ref[:, 0:256] = core[0:128]
    out_ref[:, 256:384] = core[128:256, 128:256]
    out_ref[:, 384:512] = jnp.zeros((128, 128), F32)
    out_ref[0:8, 384:512] = extra


def summed_body(parts_ref, out_ref):
    out_ref[...] = jnp.broadcast_to(jnp.sum(parts_ref[...], axis=0, keepdims=True), out_ref.shape)


def inverted(work_ref):
    size = work_ref.shape[0]
    panels = size // 8
    sub = lax.broadcasted_iota(jnp.int32, (8, 1), 0)
    lanes = lax.broadcasted_iota(jnp.int32, (1, size), 1)

    def column(block, step, j):
        index = jnp.full((8, 128), 0, jnp.int32) + ((step % 16) * 8 + j)
        window = jnp.where(step < 16, block[:, 0:128], block[:, 128:256])
        return jnp.take_along_axis(window, index, axis=1)

    def wide(value):
        return jnp.concatenate([value, value], axis=1)

    def eliminated(panel, step):
        diag = [column(panel, step, j) for j in range(8)]
        for j in range(8):
            inverse = 1.0 / diag[j][j : j + 1, :]
            for k in range(j + 1, 8):
                pivot = diag[k][j : j + 1, :] * inverse
                diag[k] = jnp.where(sub == j, pivot, diag[k] - diag[j] * pivot)
            panel = jnp.where(lanes == step * 8 + j, jnp.where(sub == j, 1.0, 0.0), panel)
            row = panel[j : j + 1, :] * wide(inverse)
            panel = jnp.where(sub == j, row, panel - wide(diag[j]) * row)
        return panel

    def split(value):
        return [part.astype(F32) for part in split3(value)]

    def stacked(parts):
        return jnp.concatenate(parts, axis=0).astype(BF16)

    def panel_step(step, carry):
        panel, factors = carry
        following = jnp.minimum(step + 1, panels - 1)
        here = pl.ds(pl.multiple_of(step * 8, 8), 8)
        ahead = work_ref[pl.ds(pl.multiple_of(following * 8, 8), 8), :]
        inside = (lanes >= step * 8) & (lanes < step * 8 + 8)
        following_rows = jnp.where(inside, 0.0, ahead)
        for j in range(8):
            following_rows = following_rows - wide(column(ahead, step, j)) * panel[j : j + 1, :]
        f1, f2, f3 = split(factors)
        p1, p2, p3 = split(panel)
        update = lax.dot_general(
            stacked([f1, f1, f2, f2, f1, f3]),
            stacked([p1, p2, p1, p2, p3, p1]),
            (((0,), (0,)), ((), ())),
            preferred_element_type=F32,
        )
        work_ref[...] = jnp.where(inside, 0.0, work_ref[...]) - update
        work_ref[here, :] = panel
        following_factors = jnp.where(lanes < following * 8, -following_rows, following_rows)
        return eliminated(following_rows, following), following_factors

    start = work_ref[0:8, :]
    lax.fori_loop(0, panels, panel_step, (eliminated(start, 0), start))


def eight(row):
    return jnp.broadcast_to(row, (8, row.shape[1]))


def row_dot(a, b):
    return jnp.sum(a * b, axis=1, keepdims=True)


def times(vector, matrix, transposed=False):
    dims = (((1,), (1 if transposed else 0,)), ((), ()))
    return lax.dot_general(vector, matrix, dims, precision=HIGH, preferred_element_type=F32)


def first_body(packed_ref, sketch_ref, targets_ref, ridge_ref, inverse_ref, state_ref, send_ref):
    inverse_ref[0:128, :] = packed_ref[:, 0:256]
    inverse_ref[128:256, 0:128] = packed_ref[:, 128:256].T
    inverse_ref[128:256, 128:256] = packed_ref[:, 256:384]
    inverted(inverse_ref)
    projected = jnp.concatenate([packed_ref[0:1, 384:512], packed_ref[1:2, 384:512]], axis=1)
    square = packed_ref[2:3, 384:385]
    solved = times(eight(projected), inverse_ref[...])
    fitted = times(solved, sketch_ref[...], transposed=True)
    ridge = ridge_ref[0, 0]
    direction = (targets_ref[...] - fitted[0:1]) / ridge
    descent = (square - row_dot(projected, solved[0:1])) / ridge
    state_ref[0:1, :] = direction
    state_ref[1:2, :] = projected
    state_ref[2:3, :] = jnp.broadcast_to(square, (1, 256))
    state_ref[3:4, :] = jnp.broadcast_to(descent, (1, 256))
    send_ref[...] = jnp.broadcast_to(direction, send_ref.shape)


def products(kern_refs, vector):
    tiles = kern_refs[0].shape[1] // 128
    sub = lax.broadcasted_iota(jnp.int32, (8, 128), 0)
    lane = lax.broadcasted_iota(jnp.int32, (8, 128), 1)
    chip, core = lax.axis_index("col_0"), lax.axis_index("col_1")
    chips = len(kern_refs)
    for shift, kern_ref in zip(ORDER, kern_refs):
        for flip in range(2):
            place = (chip + (chips - shift)) % chips * 2 + (core + flip) % 2
            for half in range(2):
                packed = jnp.zeros((8, 128), F32)
                for start in range(0, 128, 64):
                    base = flip * 256 + half * 128 + start
                    acc = [None] * 8
                    for k in range(tiles):
                        span = slice(k % 2 * 128, k % 2 * 128 + 128)
                        piece = eight(vector[k // 2 : k // 2 + 1, span])
                        for g in range(8):
                            block = kern_ref[
                                base + g * 8 : base + g * 8 + 8, k * 128 : k * 128 + 128
                            ]
                            acc[g] = block * piece if k == 0 else acc[g] + block * piece
                    for g in range(8):
                        total = jnp.sum(acc[g], axis=1, keepdims=True)
                        packed = packed + jnp.where(lane == sub + (start + g * 8), total, 0.0)
                yield place, half, jnp.sum(packed, axis=0, keepdims=True)


def product_body(*refs):
    *kern_refs, vector_ref, out_ref = refs
    for place, half, piece in products(kern_refs, vector_ref):
        out_ref[place, :, half * 128 : half * 128 + 128] = eight(piece)


def last_product_body(*refs):
    *kern_refs, vector_ref, out_ref = refs
    rows = out_ref.shape[0] // 8
    own_place = lax.axis_index("col_0") * 2 + lax.axis_index("col_1")
    own_row = lax.axis_index("row_0") * 4 + lax.axis_index("row_1")
    mine = lax.broadcasted_iota(jnp.int32, (rows, 128), 0) == own_row
    curve = jnp.zeros((rows, 128), F32)

    def group(place):
        return pl.ds(pl.multiple_of(place * rows, rows), rows)

    for place, half, piece in products(kern_refs, vector_ref[group(own_place), :]):
        span = slice(half * 128, half * 128 + 128)
        curve = curve + piece * jnp.where(mine, vector_ref[group(place), span], 0.0)
        out_ref[group(place), span] = jnp.broadcast_to(piece, (rows, 128))
    curve = jnp.sum(curve, axis=0, keepdims=True)
    out_ref[:, 256:384] = jnp.broadcast_to(curve, (out_ref.shape[0], 128))


def kernel_times(kerns, vector):
    return call(product_body, shape(8, 8, 256), *kerns, vector, limit=KLIMIT2)


def image_body(parts_ref, state_ref, sketch_ref, targets_ref, ridge_ref, image_ref, send_ref):
    image = jnp.sum(parts_ref[...], axis=0)[0:1] + ridge_ref[0, 0] * state_ref[0:1, :]
    image_ref[...] = eight(image)
    along = times(eight(image), sketch_ref[...])[0:1]
    lane = lax.broadcasted_iota(jnp.int32, (1, 128), 1)
    sums = jnp.where(
        lane == 0,
        row_dot(state_ref[0:1, :], image),
        jnp.where(
            lane == 1, row_dot(image, image), jnp.where(lane == 2, row_dot(targets_ref[...], image), 0.0)
        ),
    )
    send_ref[:, 0:256] = jnp.broadcast_to(along, (send_ref.shape[0], 256))
    send_ref[:, 256:384] = jnp.broadcast_to(sums, (send_ref.shape[0], 128))


def second_body(
    parts_ref, state_ref, image_ref, inverse_ref, sketch_ref, targets_ref, ridge_ref, next_ref, send_ref
):
    sums = jnp.sum(parts_ref[...], axis=0, keepdims=True)
    along = sums[:, 0:256]
    curve, image_square, cross = sums[:, 256:257], sums[:, 257:258], sums[:, 258:259]
    ridge = ridge_ref[0, 0]
    descent = state_ref[3:4, :]
    step = descent / curve
    projected = state_ref[1:2, :] - step * along
    solved = times(eight(projected), inverse_ref[...])
    fitted = times(solved, sketch_ref[...], transposed=True)[0:1]
    resid = targets_ref[...] - step * image_ref[0:1, :]
    square = state_ref[2:3, :] - 2.0 * step * cross + step * step * image_square
    fresh = (square - row_dot(projected, solved[0:1])) / ridge
    direction = (resid - fitted) / ridge + fresh / descent * state_ref[0:1, :]
    next_ref[0:1, :] = direction
    next_ref[1:2, :] = step
    next_ref[2:3, :] = fresh
    send_ref[...] = jnp.broadcast_to(direction, send_ref.shape)


def finish_body(
    parts_ref,
    every_ref,
    state_ref,
    next_ref,
    image_ref,
    targets_ref,
    ridge_ref,
    coefficients_ref,
    residual_ref,
):
    ridge = ridge_ref[0, 0]
    own_row = lax.axis_index("row_0") * 4 + lax.axis_index("row_1")
    rows = parts_ref.shape[0] // 8
    direction = next_ref[0:1, :]
    mine = lax.broadcasted_iota(jnp.int32, (8 * rows, 256), 0) % rows == own_row
    last = jnp.sum(jnp.where(mine, parts_ref[:, 0:256], 0.0), axis=0, keepdims=True)
    last = last + ridge * direction
    every = every_ref[...]
    square = jnp.sum(jnp.sum(every * every, axis=0, keepdims=True), axis=1, keepdims=True)
    curve = jnp.sum(
        jnp.sum(parts_ref[:, 256:384], axis=0, keepdims=True), axis=1, keepdims=True
    )
    step = next_ref[1:2, :]
    last_step = next_ref[2:3, :] / (curve + ridge * square)
    coefficients_ref[...] = step * state_ref[0:1, :] + last_step * direction
    residual_ref[...] = targets_ref[...] - step * image_ref[0:1, :] - last_step * last


def local(points, feature_scale, test_matrix, targets, ridge):
    everyone = lax.axis_size(COL_ROW)
    row_devices = lax.axis_size(ROW)
    own, rank = test_matrix.shape
    ridge = ridge.reshape(1, 1)
    targets = targets.reshape(1, own)
    scale = feature_scale.reshape(1, -1)
    parts, copies = call(
        parts_body,
        [shape(own, 128, dtype=BF16), shape(row_devices, own, 128 + rank, dtype=BF16)],
        points,
        scale,
        test_matrix,
    )
    chips, cores = lax.axis_size("col_0"), lax.axis_size("col_1")
    chunks = {}
    for shift in range(chips):
        for flip in range(cores):
            pairs = [
                (c, (c // 2 + shift) % chips * 2 + (c % 2 ^ flip)) for c in range(chips * cores)
            ]
            chunks[shift, flip] = lax.ppermute(parts, COL, pairs) if shift or flip else parts
    message = exchanged(copies, ROW).reshape(-1, 128 + rank)
    early = {key: value for key, value in chunks.items() if key not in LATE}
    message, early = lax.optimization_barrier((message, early))
    chunks.update(early)
    norm = call(norms_body, shape(8, message.shape[0]), message)
    kerns, partial, sent = [], [], []
    for number, shift in enumerate(ORDER):
        first = chunks[shift, 0]
        if number > 1:
            first, partial[number - 2] = lax.optimization_barrier((first, partial[number - 2]))
        kern, near, other = kernel_block(first, chunks[shift, 1], message, norm)
        kerns.append(kern)
        swapped = lax.ppermute(other, "col_1", [(0, 1), (1, 0)])
        partial.append(near + swapped if shift else (near, swapped))
    for number, shift in enumerate(ORDER[:-1]):
        pairs = [(c, (c - shift) % chips) for c in range(chips)]
        sent.append(lax.ppermute(partial[number], "col_0", pairs))
    sums = [*partial[-1], *sent]
    sketch_out, sketch, packed = call(
        core_body,
        [shape(own, rank), shape(own, rank), shape(everyone, 512)],
        *sums,
        test_matrix,
        targets,
        ridge,
    )
    packed = exchanged(packed, COL_ROW)
    packed = call(summed_body, shape(everyone, 512), packed)
    packed = exchanged(packed, COL_ROW)
    inverse, state, send = call(
        first_body,
        [shape(rank, rank), shape(8, own), shape(row_devices, own)],
        packed,
        sketch,
        targets,
        ridge,
    )
    product = kernel_times(kerns, exchanged(send, ROW))
    image, send = call(
        image_body,
        [shape(8, own), shape(everyone, 384)],
        exchanged(product, COL),
        state,
        sketch,
        targets,
        ridge,
    )
    following, send = call(
        second_body,
        [shape(8, own), shape(everyone, own)],
        exchanged(send, COL_ROW),
        state,
        image,
        inverse,
        sketch,
        targets,
        ridge,
    )
    every = exchanged(send, COL_ROW)
    product = call(last_product_body, shape(everyone, 384), *kerns, every, limit=KLIMIT2)
    coefficients, residual = call(
        finish_body,
        [shape(1, own), shape(1, own)],
        exchanged(product, COL_ROW),
        every,
        state,
        following,
        image,
        targets,
        ridge,
    )
    return coefficients.reshape(own), residual.reshape(own), sketch_out


def solution(mesh):
    split = Mesh(mesh.devices.reshape(4, 4, 4, 2), ROW + COL)

    return jax.shard_map(
        local,
        mesh=split,
        in_specs=(P(COL_ROW, None), P(), P(COL_ROW, None), P(COL_ROW), P()),
        out_specs=(P(COL_ROW), P(COL_ROW), P(COL_ROW, None)),
        check_vma=False,
    )
```

profile of v0, /device:TPU:1, one launch (start us, length us, event | category | flops | bytes accessed | tf_op | source)
XLA Modules:
  0.0 206.7 jit_solution(6206219724624691392)
XLA Ops:
  0.6 0.9 copy.9.points_ref
  3.5 1.6 copy-done
  5.1 8.6 %all-to-all-start = ((bf16[16,256,384]{2,1,0:T(8,128)(2,1)}), bf16[16,256,384]{2,1,0:T(8,128)(2,1)S(1)}, u32[]{:S(2)}, u32[]{:S(2)}) async-start(bf16[16,256,384]{2,1,0:T(8,128)(2,1)} %copy-done), calls=%async_computation | async-start | bytes 6291456 | tf_op jit(solution)/shard_map/all_to_all | solution.py:41
  13.7 1.3 collective-permute-start
  15.0 2.3 %collective-permute-start.1 = (bf16[256,128]{1,0:T(8,128)(2,1)S(1)}, bf16[256,128]{1,0:T(8,128)(2,1)S(1)}, u32[]{:S(2)}, u32[]{:S(2)}) collective-permute-start(bf16[256,128]{1,0:T(8,128)(2,1)S(1)} %get-tuple-element.57.first_ref), channel_id=1, source_target_pairs={{0,3},{1,2},{2,5},{3,4},{4,7},{5,6},{6,1},{7,0},{8,11},{9,10},{10,... | collective-permute-start | bytes 196616 | tf_op jit(solution)/shard_map/ppermute | solution.py:380
  17.3 1.4 collective-permute-start.2
  18.8 1.0 collective-permute-start.3
  19.7 1.5 collective-permute-start.4
  21.2 1.7 collective-permute-done.2.first_ref
  23.0 1.7 collective-permute-done.3.second_ref
  24.6 29.4 %all-to-all-done = bf16[16,256,384]{2,1,0:T(8,128)(2,1)S(1)} async-done(((bf16[16,256,384]{2,1,0:T(8,128)(2,1)}), bf16[16,256,384]{2,1,0:T(8,128)(2,1)S(1)}, u32[]{:S(2)}, u32[]{:S(2)}) %all-to-all-start) | async-done | bytes 3145760 | tf_op jit(solution)/shard_map/all_to_all | solution.py:41
  54.9 2.9 %shard_map.78 = (f32[512,4096]{1,0:T(8,128)S(1)}, f32[256,256]{1,0:T(8,128)S(1)}, f32[256,256]{1,0:T(8,128)S(1)}) custom-call(bf16[256,128]{1,0:T(8,128)(2,1)S(1)} %collective-permute-done.2.first_ref, bf16[256,128]{1,0:T(8,128)(2,1)S(1)} %collective-permute-done.3.second_ref, bf16[4096,384]{1,0:T(8,128)(2,1)S(1)} %bitcast.36, f32[8,4096]{1,0:T(8,128)S(1)} %shard_map.77.norm_ref), custom_call_target="tpu_custom_call" | custom-call | tf_op jit(solution)/shard_map/pallas_call | solution.py:28
  57.8 3.1 %collective-permute-start.5 = (f32[256,256]{1,0:T(8,128)S(1)}, f32[256,256]{1,0:T(8,128)S(1)}, u32[]{:S(2)}, u32[]{:S(2)}) collective-permute-start(f32[256,256]{1,0:T(8,128)S(1)} %get-tuple-element.51), channel_id=1, source_target_pairs={{0,1},{1,0},{2,3},{3,2},{4,5},{5,4},{6,7},{7,6},{8,9},{9,8},{10,11... | collective-permute-start | bytes 786440 | tf_op jit(solution)/shard_map/ppermute | solution.py:393
  60.9 2.4 %collective-permute-start.6 = (bf16[256,128]{1,0:T(8,128)(2,1)S(1)}, bf16[256,128]{1,0:T(8,128)(2,1)S(1)}, u32[]{:S(2)}, u32[]{:S(2)}) collective-permute-start(bf16[256,128]{1,0:T(8,128)(2,1)S(1)} %get-tuple-element.57.first_ref), channel_id=1, source_target_pairs={{0,7},{1,6},{2,1},{3,0},{4,3},{5,2},{6,5},{7,4},{8,15},{9,14},{10,... | collective-permute-start | bytes 196616 | tf_op jit(solution)/shard_map/ppermute | solution.py:380
  63.3 2.9 %shard_map.79 = (f32[512,4096]{1,0:T(8,128)S(1)}, f32[256,256]{1,0:T(8,128)S(1)}, f32[256,256]{1,0:T(8,128)S(1)}) custom-call(bf16[256,128]{1,0:T(8,128)(2,1)S(1)} %collective-permute-done.first_ref, bf16[256,128]{1,0:T(8,128)(2,1)S(1)} %collective-permute-done.1.second_ref, bf16[4096,384]{1,0:T(8,128)(2,1)S(1)} %bitcast.37, f32[8,4096]{1,0:T(8,128)S(1)} %shard_map.77.norm_ref), custom_call_target="tpu_custom_call" | custom-call | tf_op jit(solution)/shard_map/pallas_call | solution.py:28
  66.9 2.9 %shard_map.80 = (f32[512,4096]{1,0:T(8,128)S(1)}, f32[256,256]{1,0:T(8,128)S(1)}, f32[256,256]{1,0:T(8,128)S(1)}) custom-call(bf16[256,128]{1,0:T(8,128)(2,1)S(1)} %collective-permute-done.4.first_ref, bf16[256,128]{1,0:T(8,128)(2,1)S(1)} %collective-permute-done.6.second_ref, bf16[4096,384]{1,0:T(8,128)(2,1)S(1)} %bitcast.38, f32[8,4096]{1,0:T(8,128)S(1)} %shard_map.77.norm_ref), custom_call_target="tpu_custom_call" | custom-call | tf_op jit(solution)/shard_map/pallas_call | solution.py:28
  70.4 1.1 collective-permute-done.8.second_ref
  71.5 2.9 %shard_map.81 = (f32[512,4096]{1,0:T(8,128)S(1)}, f32[256,256]{1,0:T(8,128)S(1)}, f32[256,256]{1,0:T(8,128)S(1)}) custom-call(bf16[256,128]{1,0:T(8,128)(2,1)S(1)} %get-tuple-element.57.first_ref, bf16[256,128]{1,0:T(8,128)(2,1)S(1)} %collective-permute-done.8.second_ref, bf16[4096,384]{1,0:T(8,128)(2,1)S(1)} %bitcast.39, f32[8,4096]{1,0:T(8,128)S(1)} %shard_map.77.norm_ref), custom_call_target="tpu_custom_call" | custom-call | tf_op jit(solution)/shard_map/pallas_call | solution.py:28
  74.5 1.4 collective-permute-start.11
  77.4 4.7 %collective-permute-done.11.two_ref = f32[256,256]{1,0:T(8,128)S(1)} collective-permute-done((f32[256,256]{1,0:T(8,128)S(1)}, f32[256,256]{1,0:T(8,128)S(1)}, u32[]{:S(2)}, u32[]{:S(2)}) %collective-permute-start.11) | collective-permute-done | bytes 262176 | tf_op jit(solution)/shard_map/ppermute | solution.py:397
  82.0 2.7 %collective-permute-done.10.one_ref = f32[256,256]{1,0:T(8,128)S(1)} collective-permute-done((f32[256,256]{1,0:T(8,128)S(1)}, f32[256,256]{1,0:T(8,128)S(1)}, u32[]{:S(2)}, u32[]{:S(2)}) %collective-permute-start.10) | collective-permute-done | bytes 262176 | tf_op jit(solution)/shard_map/ppermute | solution.py:397
  84.8 6.2 %collective-permute-done.13.three_ref = f32[256,256]{1,0:T(8,128)S(1)} collective-permute-done((f32[256,256]{1,0:T(8,128)S(1)}, f32[256,256]{1,0:T(8,128)S(1)}, u32[]{:S(2)}, u32[]{:S(2)}) %collective-permute-start.13) | collective-permute-done | bytes 262176 | tf_op jit(solution)/shard_map/ppermute | solution.py:397
  92.1 19.3 %all_to_all.76 = f32[128,1,512]{2,1,0:T(1,128)S(1)} all-to-all(f32[128,1,512]{2,1,0:T(1,128)S(1)} %copy.10), channel_id=1, replica_groups=mesh['row_0'=4,'row_1'=4,'col_0'=4,'col_1'=2] {'col_0','col_1','row_0','..., dimensions={0} | all-to-all | bytes 524288 | tf_op jit(solution)/shard_map/all_to_all | solution.py:41
  111.7 15.2 %all_to_all.77 = f32[128,1,512]{2,1,0:T(1,128)S(1)} all-to-all(f32[128,1,512]{2,1,0:T(1,128)S(1)} %copy.11), channel_id=1, replica_groups=mesh['row_0'=4,'row_1'=4,'col_0'=4,'col_1'=2] {'col_0','col_1','row_0','..., dimensions={0} | all-to-all | bytes 524288 | tf_op jit(solution)/shard_map/all_to_all | solution.py:41
  127.0 9.6 %shard_map.84 = (f32[256,256]{1,0:T(8,128)S(1)}, f32[8,256]{1,0:T(8,128)S(1)}, f32[16,256]{1,0:T(8,128)S(1)}) custom-call(f32[128,512]{1,0:T(8,128)S(1)} %bitcast.42, f32[256,256]{1,0:T(8,128)S(1)} %get-tuple-element.66.sketch_ref, f32[1,256]{1,0:T(1,128)S(1)} %bitcast.53, f32[1,1]{1,0:T(1,128)} %bitcast.31.ridge_ref), custom_call_target="tpu_custom_call" | custom-call | tf_op jit(solution)/shard_map/pallas_call | solution.py:28
  136.7 9.1 %all_to_all.78 = f32[16,1,256]{2,1,0:T(1,128)S(1)} all-to-all(f32[16,1,256]{2,1,0:T(1,128)S(1)} %copy.12), channel_id=1, replica_groups=mesh['row_0'=4,'row_1'=4,'col_0'=4,'col_1'=2] {'row_0','row_1'}, dimensions={0} | all-to-all | bytes 32768 | tf_op jit(solution)/shard_map/all_to_all | solution.py:41
  145.7 2.9 %shard_map.85 = f32[8,8,256]{2,1,0:T(8,128)S(1)} custom-call(f32[512,4096]{1,0:T(8,128)S(1)} %get-tuple-element.45.refs_0_, f32[512,4096]{1,0:T(8,128)S(1)} %get-tuple-element.48.refs_1_, f32[512,4096]{1,0:T(8,128)S(1)} %get-tuple-element.53.refs_2_, f32[512,4096]{1,0:T(8,128)S(1)} %get-tuple-element.58.refs_3_, f32[16,256]{1,0:T(8,128)S(1)} %bitcast.51), custom_call_target="tpu_custom_call" | custom-call | tf_op jit(solution)/shard_map/pallas_call | solution.py:28
  148.7 9.5 %all_to_all.79.parts_ref = f32[8,8,256]{2,1,0:T(8,128)S(1)} all-to-all(f32[8,8,256]{2,1,0:T(8,128)S(1)} %shard_map.85), channel_id=1, replica_groups=mesh['row_0'=4,'row_1'=4,'col_0'=4,'col_1'=2] {'col_0','col_1'}, dimensions={0} | all-to-all | bytes 131072 | tf_op jit(solution)/shard_map/all_to_all | solution.py:41
  158.6 14.5 %all_to_all.80 = f32[128,1,384]{2,1,0:T(1,128)S(1)} all-to-all(f32[128,1,384]{2,1,0:T(1,128)S(1)} %copy.13), channel_id=1, replica_groups=mesh['row_0'=4,'row_1'=4,'col_0'=4,'col_1'=2] {'col_0','col_1','row_0','..., dimensions={0} | all-to-all | bytes 393216 | tf_op jit(solution)/shard_map/all_to_all | solution.py:41
  174.1 14.2 %all_to_all.81 = f32[128,1,256]{2,1,0:T(1,128)S(1)} all-to-all(f32[128,1,256]{2,1,0:T(1,128)S(1)} %copy.14), channel_id=1, replica_groups=mesh['row_0'=4,'row_1'=4,'col_0'=4,'col_1'=2] {'col_0','col_1','row_0','..., dimensions={0} | all-to-all | bytes 262144 | tf_op jit(solution)/shard_map/all_to_all | solution.py:41
  188.3 2.9 %shard_map.88 = f32[128,384]{1,0:T(8,128)S(1)} custom-call(f32[512,4096]{1,0:T(8,128)S(1)} %get-tuple-element.45.refs_0_, f32[512,4096]{1,0:T(8,128)S(1)} %get-tuple-element.48.refs_1_, f32[512,4096]{1,0:T(8,128)S(1)} %get-tuple-element.53.refs_2_, f32[512,4096]{1,0:T(8,128)S(1)} %get-tuple-element.58.refs_3_, f32[128,256]{1,0:T(8,128)S(1)} %bitcast.40), custom_call_target="tpu_custom_call" | custom-call | tf_op jit(solution)/shard_map/pallas_call | solution.py:28
  191.4 14.6 %all_to_all.82 = f32[128,1,384]{2,1,0:T(1,128)S(1)} all-to-all(f32[128,1,384]{2,1,0:T(1,128)S(1)} %copy.15), channel_id=1, replica_groups=mesh['row_0'=4,'row_1'=4,'col_0'=4,'col_1'=2] {'col_0','col_1','row_0','..., dimensions={0} | all-to-all | bytes 393216 | tf_op jit(solution)/shard_map/all_to_all | solution.py:41
  (45 shorter events, 8.8 us)
Async XLA Ops:
  1.6 0.9 copy-start.1
  2.5 0.7 copy-start.4
  3.5 1.6 copy-start
  5.1 48.9 %all-to-all-start = ((bf16[16,256,384]{2,1,0:T(8,128)(2,1)}), bf16[16,256,384]{2,1,0:T(8,128)(2,1)S(1)}, u32[]{:S(2)}, u32[]{:S(2)}) async-start(bf16[16,256,384]{2,1,0:T(8,128)(2,1)} %copy-done), calls=%async_computation | async-start | bytes 6291456 | tf_op jit(solution)/shard_map/all_to_all | solution.py:41
  13.7 7.5 %collective-permute-start = (bf16[256,128]{1,0:T(8,128)(2,1)S(1)}, bf16[256,128]{1,0:T(8,128)(2,1)S(1)}, u32[]{:S(2)}, u32[]{:S(2)}) collective-permute-start(bf16[256,128]{1,0:T(8,128)(2,1)S(1)} %get-tuple-element.57.first_ref), channel_id=1, source_target_pairs={{0,2},{1,3},{2,4},{3,5},{4,6},{5,7},{6,0},{7,1},{8,10},{9,11},{10,... | collective-permute-start | bytes 196616 | tf_op jit(solution)/shard_map/ppermute | solution.py:380
  15.0 6.2 %collective-permute-start.1 = (bf16[256,128]{1,0:T(8,128)(2,1)S(1)}, bf16[256,128]{1,0:T(8,128)(2,1)S(1)}, u32[]{:S(2)}, u32[]{:S(2)}) collective-permute-start(bf16[256,128]{1,0:T(8,128)(2,1)S(1)} %get-tuple-element.57.first_ref), channel_id=1, source_target_pairs={{0,3},{1,2},{2,5},{3,4},{4,7},{5,6},{6,1},{7,0},{8,11},{9,10},{10,... | collective-permute-start | bytes 196616 | tf_op jit(solution)/shard_map/ppermute | solution.py:380
  17.3 5.6 %collective-permute-start.2 = (bf16[256,128]{1,0:T(8,128)(2,1)S(1)}, bf16[256,128]{1,0:T(8,128)(2,1)S(1)}, u32[]{:S(2)}, u32[]{:S(2)}) collective-permute-start(bf16[256,128]{1,0:T(8,128)(2,1)S(1)} %get-tuple-element.57.first_ref), channel_id=1, source_target_pairs={{0,4},{1,5},{2,6},{3,7},{4,0},{5,1},{6,2},{7,3},{8,12},{9,13},{10,... | collective-permute-start | bytes 196616 | tf_op jit(solution)/shard_map/ppermute | solution.py:380
  18.8 5.9 %collective-permute-start.3 = (bf16[256,128]{1,0:T(8,128)(2,1)S(1)}, bf16[256,128]{1,0:T(8,128)(2,1)S(1)}, u32[]{:S(2)}, u32[]{:S(2)}) collective-permute-start(bf16[256,128]{1,0:T(8,128)(2,1)S(1)} %get-tuple-element.57.first_ref), channel_id=1, source_target_pairs={{0,5},{1,4},{2,7},{3,6},{4,1},{5,0},{6,3},{7,2},{8,13},{9,12},{10,... | collective-permute-start | bytes 196616 | tf_op jit(solution)/shard_map/ppermute | solution.py:380
  19.7 4.9 %collective-permute-start.4 = (bf16[256,128]{1,0:T(8,128)(2,1)S(1)}, bf16[256,128]{1,0:T(8,128)(2,1)S(1)}, u32[]{:S(2)}, u32[]{:S(2)}) collective-permute-start(bf16[256,128]{1,0:T(8,128)(2,1)S(1)} %get-tuple-element.57.first_ref), channel_id=1, source_target_pairs={{0,6},{1,7},{2,0},{3,1},{4,2},{5,3},{6,4},{7,5},{8,14},{9,15},{10,... | collective-permute-start | bytes 196616 | tf_op jit(solution)/shard_map/ppermute | solution.py:380
  54.9 36.1 %copy-start.2 = (bf16[256,256]{1,0:T(8,128)(2,1)S(1)}, bf16[256,256]{1,0:T(8,128)(2,1)}, u32[]{:S(2)}) copy-start(bf16[256,256]{1,0:T(8,128)(2,1)} %test_ref.3) | copy-start | bytes 393220
  54.9 36.1 %copy-start.3 = (f32[256]{0:T(256)S(1)}, f32[256]{0:T(256)}, u32[]{:S(2)}) copy-start(f32[256]{0:T(256)} %param.8) | copy-start | bytes 3076
  57.8 9.1 %collective-permute-start.5 = (f32[256,256]{1,0:T(8,128)S(1)}, f32[256,256]{1,0:T(8,128)S(1)}, u32[]{:S(2)}, u32[]{:S(2)}) collective-permute-start(f32[256,256]{1,0:T(8,128)S(1)} %get-tuple-element.51), channel_id=1, source_target_pairs={{0,1},{1,0},{2,3},{3,2},{4,5},{5,4},{6,7},{7,6},{8,9},{9,8},{10,11... | collective-permute-start | bytes 786440 | tf_op jit(solution)/shard_map/ppermute | solution.py:393
  60.9 6.0 %collective-permute-start.6 = (bf16[256,128]{1,0:T(8,128)(2,1)S(1)}, bf16[256,128]{1,0:T(8,128)(2,1)S(1)}, u32[]{:S(2)}, u32[]{:S(2)}) collective-permute-start(bf16[256,128]{1,0:T(8,128)(2,1)S(1)} %get-tuple-element.57.first_ref), channel_id=1, source_target_pairs={{0,7},{1,6},{2,1},{3,0},{4,3},{5,2},{6,5},{7,4},{8,15},{9,14},{10,... | collective-permute-start | bytes 196616 | tf_op jit(solution)/shard_map/ppermute | solution.py:380
  66.2 4.2 %collective-permute-start.7 = (f32[256,256]{1,0:T(8,128)S(1)}, f32[256,256]{1,0:T(8,128)S(1)}, u32[]{:S(2)}, u32[]{:S(2)}) collective-permute-start(f32[256,256]{1,0:T(8,128)S(1)} %get-tuple-element.56), channel_id=1, source_target_pairs={{0,1},{1,0},{2,3},{3,2},{4,5},{5,4},{6,7},{7,6},{8,9},{9,8},{10,11... | collective-permute-start | bytes 786440 | tf_op jit(solution)/shard_map/ppermute | solution.py:393
  69.8 6.2 %collective-permute-start.12 = (f32[256,256]{1,0:T(8,128)S(1)}, f32[256,256]{1,0:T(8,128)S(1)}, u32[]{:S(2)}, u32[]{:S(2)}) collective-permute-start(f32[256,256]{1,0:T(8,128)S(1)} %get-tuple-element.64), channel_id=1, source_target_pairs={{0,1},{1,0},{2,3},{3,2},{4,5},{5,4},{6,7},{7,6},{8,9},{9,8},{10,11... | collective-permute-start | bytes 786440 | tf_op jit(solution)/shard_map/ppermute | solution.py:393
  69.9 1.5 collective-permute-start.8
  74.3 3.0 %collective-permute-start.9 = (f32[256,256]{1,0:T(8,128)S(1)}, f32[256,256]{1,0:T(8,128)S(1)}, u32[]{:S(2)}, u32[]{:S(2)}) collective-permute-start(f32[256,256]{1,0:T(8,128)S(1)} %get-tuple-element.60), channel_id=1, source_target_pairs={{0,1},{1,0},{2,3},{3,2},{4,5},{5,4},{6,7},{7,6},{8,9},{9,8},{10,11... | collective-permute-start | bytes 786440 | tf_op jit(solution)/shard_map/ppermute | solution.py:393
  74.5 7.5 %collective-permute-start.11 = (f32[256,256]{1,0:T(8,128)S(1)}, f32[256,256]{1,0:T(8,128)S(1)}, u32[]{:S(2)}, u32[]{:S(2)}) collective-permute-start(f32[256,256]{1,0:T(8,128)S(1)} %add.10), channel_id=1, source_target_pairs={{0,6},{2,0},{4,2},{6,4},{1,7},{3,1},{5,3},{7,5},{8,14},{10,8},{12,... | collective-permute-start | bytes 786440 | tf_op jit(solution)/shard_map/ppermute | solution.py:397
  76.0 8.8 %collective-permute-start.10 = (f32[256,256]{1,0:T(8,128)S(1)}, f32[256,256]{1,0:T(8,128)S(1)}, u32[]{:S(2)}, u32[]{:S(2)}) collective-permute-start(f32[256,256]{1,0:T(8,128)S(1)} %add.9), channel_id=1, source_target_pairs={{0,4},{2,6},{4,0},{6,2},{1,5},{3,7},{5,1},{7,3},{8,12},{10,14},{12... | collective-permute-start | bytes 786440 | tf_op jit(solution)/shard_map/ppermute | solution.py:397
  76.0 14.9 %collective-permute-start.13 = (f32[256,256]{1,0:T(8,128)S(1)}, f32[256,256]{1,0:T(8,128)S(1)}, u32[]{:S(2)}, u32[]{:S(2)}) collective-permute-start(f32[256,256]{1,0:T(8,128)S(1)} %add.11), channel_id=1, source_target_pairs={{0,2},{2,4},{4,6},{6,0},{1,3},{3,5},{5,7},{7,1},{8,10},{10,12},{12... | collective-permute-start | bytes 786440 | tf_op jit(solution)/shard_map/ppermute | solution.py:397
where the time goes:
time: 207 us
  blocking collectives  96.3 us (47%)
  waiting for transfers between devices  47.5 us (23%)
  Pallas kernels  30.7 us (15%)
  starting transfers between devices  25.2 us (12%)
  local copies, waits for them, and re-layouts  5.33 us (3%)
    all_to_all x7, blocking collectives, exchanged(): return lax.all_to_all(pieces, axes, 0, 0, tiled=True)  96.3 us
    pallas_call x14, Pallas kernels, call(): pl.pallas_call(body, out_shape=outs, scratch_shapes=list(scratch), compil...  30.7 us
    all_to_all x1, waiting for transfers between devices, exchanged(): return lax.all_to_all(pieces, axes, 0, 0, tiled=True)  29.4 us
    ppermute x3, waiting for transfers between devices, local(): sent.append(lax.ppermute(partial[number], 'col_0', pairs))  13.6 us
    ppermute x7, starting transfers between devices, local(): lax.ppermute(parts, COL, pairs)  10.4 us
    all_to_all x1, starting transfers between devices, exchanged(): return lax.all_to_all(pieces, axes, 0, 0, tiled=True)  8.59 us
    ppermute x7, waiting for transfers between devices, local(): lax.ppermute(parts, COL, pairs)  4.51 us
    unnamed x17, local copies, waits for them, and re-layouts  4.2 us
  transfers between devices with their start and end apart: 15, of which 7 were waited for; matrix products, arithmetic and copies ran while one was open for 0% of the time, Pallas kernels for 4%

commit v1 on v0

--- a/solution.py
+++ b/solution.py
@@ -49,15 +49,55 @@
     return first, second, third
 
 
-def parts_body(points_ref, scale_ref, test_ref, out_ref, copies_ref):
-    y = points_ref[...] * (scale_ref[...] * LOG2E**0.5)
+def parts_body(
+    points_ref, scale_ref, test_ref, out_ref, copies_ref, points_scr, scale_scr, message_scr, in_sem, out_sem
+):
+    inputs = (
+        (points_ref, points_scr),
+        (scale_ref, scale_scr),
+        (test_ref, message_scr.at[:, 128:384]),
+    )
+    loads = [pltpu.make_async_copy(*pair, in_sem.at[i]) for i, pair in enumerate(inputs)]
+    for load in loads:
+        load.start()
+    loads[0].wait()
+    loads[1].wait()
+    y = points_scr[...].T * (scale_scr[...] * LOG2E**0.5)
     first = y.astype(BF16).astype(F32)
     second = (y - first).astype(BF16).astype(F32)
     parts = jnp.concatenate([first, second], axis=1).astype(BF16)
     out_ref[...] = parts
-    for i in range(copies_ref.shape[0]):
-        copies_ref[i, :, 0:128] = parts
-        copies_ref[i, :, 128:384] = test_ref[...]
+    message_scr[:, 0:128] = parts
+    loads[2].wait()
+    stores = [
+        pltpu.make_async_copy(message_scr, copies_ref.at[i], out_sem.at[i])
+        for i in range(copies_ref.shape[0])
+    ]
+    for store in stores:
+        store.start()
+    for store in stores:
+        store.wait()
+
+
+def parts_and_copies(points, scale, test, copies):
+    own, features = points.shape
+    lanes = 128 + test.shape[1]
+    anywhere = pl.BlockSpec(memory_space=pltpu.HBM)
+    return pl.pallas_call(
+        parts_body,
+        in_specs=[anywhere] * 3,
+        out_specs=[pl.BlockSpec(memory_space=pltpu.VMEM), anywhere],
+        out_shape=[shape(own, 128, dtype=BF16), pltpu.HBM((copies, own, lanes), BF16)],
+        scratch_shapes=[
+            pltpu.VMEM((features, own), F32),
+            pltpu.VMEM((1, features), F32),
+            pltpu.VMEM((own, lanes), BF16),
+            pltpu.SemaphoreType.DMA((3,)),
+            pltpu.SemaphoreType.DMA((copies,)),
+        ],
+        compiler_params=pltpu.CompilerParams(vmem_limit_bytes=4 * MIB),
+        name="parts",
+    )(*(pltpu.with_memory_space_constraint(a, pltpu.HBM) for a in (points.T, scale, test)))
 
 
 def norms_body(message_ref, norm_ref):
@@ -158,14 +198,24 @@
 
     def eliminated(panel, step):
         diag = [column(panel, step, j) for j in range(8)]
-        for j in range(8):
-            inverse = 1.0 / diag[j][j : j + 1, :]
-            for k in range(j + 1, 8):
-                pivot = diag[k][j : j + 1, :] * inverse
-                diag[k] = jnp.where(sub == j, pivot, diag[k] - diag[j] * pivot)
-            panel = jnp.where(lanes == step * 8 + j, jnp.where(sub == j, 1.0, 0.0), panel)
-            row = panel[j : j + 1, :] * wide(inverse)
-            panel = jnp.where(sub == j, row, panel - wide(diag[j]) * row)
+        for j in range(0, 8, 2):
+            a, b = diag[j][j : j + 1, :], diag[j + 1][j : j + 1, :]
+            c, d = diag[j][j + 1 : j + 2, :], diag[j + 1][j + 1 : j + 2, :]
+            inverse = 1.0 / (a * d - b * c)
+            upper, lower = sub == j, sub == j + 1
+
+            def swept(block, first, second, spread=lambda value: value):
+                top, bottom = block[j : j + 1, :], block[j + 1 : j + 2, :]
+                new_top = (spread(d) * top - spread(b) * bottom) * spread(inverse)
+                new_bottom = (spread(a) * bottom - spread(c) * top) * spread(inverse)
+                rest = block - first * new_top - second * new_bottom
+                return jnp.where(upper, new_top, jnp.where(lower, new_bottom, rest))
+
+            for k in range(j + 2, 8):
+                diag[k] = swept(diag[k], diag[j], diag[j + 1])
+            panel = jnp.where(lanes == step * 8 + j, jnp.where(upper, 1.0, 0.0), panel)
+            panel = jnp.where(lanes == step * 8 + j + 1, jnp.where(lower, 1.0, 0.0), panel)
+            panel = swept(panel, wide(diag[j]), wide(diag[j + 1]), wide)
         return panel
 
     def split(value):
@@ -363,13 +413,7 @@
     ridge = ridge.reshape(1, 1)
     targets = targets.reshape(1, own)
     scale = feature_scale.reshape(1, -1)
-    parts, copies = call(
-        parts_body,
-        [shape(own, 128, dtype=BF16), shape(row_devices, own, 128 + rank, dtype=BF16)],
-        points,
-        scale,
-        test_matrix,
-    )
+    parts, copies = parts_and_copies(points, scale, test_matrix, row_devices)
     chips, cores = lax.axis_size("col_0"), lax.axis_size("col_1")
     chunks = {}
     for shift in range(chips):

time: 207 us -> 205 us (level)
  local copies, waits for them, and re-layouts: 5.33 us -> 1.22 us
  Pallas kernels: 30.7 us -> 33.3 us
    unnamed x17 -> x10, local copies, waits for them, and re-layouts: 4.2 us -> 0.09 us
    pallas_call x0 -> x1, Pallas kernels: none -> 2.82 us  [parts_and_copies(): pl.pallas_call(parts_body, in_specs=[anywhere] * 3, out_specs=[pl.BlockSp...]
    pallas_call x14 -> x13, Pallas kernels: 30.7 us -> 30.5 us  [call(): pl.pallas_call(body, out_shape=outs, scratch_shapes=list(scratch), compil...]
where the time goes in v1:
time: 205 us
  blocking collectives  96.2 us (47%)
  waiting for transfers between devices  47.5 us (23%)
  Pallas kernels  33.3 us (16%)
  starting transfers between devices  25.2 us (12%)
    all_to_all x7, blocking collectives, exchanged(): return lax.all_to_all(pieces, axes, 0, 0, tiled=True)  96.2 us
    pallas_call x13, Pallas kernels, call(): pl.pallas_call(body, out_shape=outs, scratch_shapes=list(scratch), compil...  30.5 us
    all_to_all x1, waiting for transfers between devices, exchanged(): return lax.all_to_all(pieces, axes, 0, 0, tiled=True)  29.4 us
    ppermute x3, waiting for transfers between devices, local(): sent.append(lax.ppermute(partial[number], 'col_0', pairs))  13.6 us
    ppermute x7, starting transfers between devices, local(): lax.ppermute(parts, COL, pairs)  10.4 us
    all_to_all x1, starting transfers between devices, exchanged(): return lax.all_to_all(pieces, axes, 0, 0, tiled=True)  8.6 us
    ppermute x7, waiting for transfers between devices, local(): lax.ppermute(parts, COL, pairs)  4.51 us
    ppermute x4, starting transfers between devices, local(): swapped = lax.ppermute(other, 'col_1', [(0, 1), (1, 0)])  4.16 us
  transfers between devices with their start and end apart: 15, of which 7 were waited for; matrix products, arithmetic and copies ran while one was open for 0% of the time, Pallas kernels for 4%

profile of v1, /device:TPU:1, one launch (start us, length us, event | category | flops | bytes accessed | tf_op | source)
XLA Modules:
  0.0 205.1 jit_solution(4290454585992917189)
XLA Ops:
  0.6 2.8 %parts.1 = (bf16[256,128]{1,0:T(8,128)(2,1)S(1)}, bf16[16,256,384]{2,1,0:T(8,128)(2,1)}) custom-call(f32[64,256]{1,0:T(8,128)} %bitcast.59, f32[1,64]{1,0:T(1,128)} %bitcast.60, bf16[256,256]{1,0:T(8,128)(2,1)} %test_ref.3), custom_call_target="tpu_custom_call" | custom-call | tf_op jit(solution)/shard_map/parts/pallas_call | solution.py:86
  3.5 8.6 %all-to-all-start = ((bf16[16,256,384]{2,1,0:T(8,128)(2,1)}), bf16[16,256,384]{2,1,0:T(8,128)(2,1)S(1)}, u32[]{:S(2)}, u32[]{:S(2)}) async-start(bf16[16,256,384]{2,1,0:T(8,128)(2,1)} %get-tuple-element.40), calls=%async_computation | async-start | bytes 6291456 | tf_op jit(solution)/shard_map/all_to_all | solution.py:41
  12.1 1.3 collective-permute-start
  13.3 2.3 %collective-permute-start.1 = (bf16[256,128]{1,0:T(8,128)(2,1)S(1)}, bf16[256,128]{1,0:T(8,128)(2,1)S(1)}, u32[]{:S(2)}, u32[]{:S(2)}) collective-permute-start(bf16[256,128]{1,0:T(8,128)(2,1)S(1)} %get-tuple-element.57.first_ref), channel_id=1, source_target_pairs={{0,3},{1,2},{2,5},{3,4},{4,7},{5,6},{6,1},{7,0},{8,11},{9,10},{10,... | collective-permute-start | bytes 196616 | tf_op jit(solution)/shard_map/ppermute | solution.py:424
  15.7 1.4 collective-permute-start.2
  17.1 1.0 collective-permute-start.3
  18.1 1.5 collective-permute-start.4
  19.6 1.7 collective-permute-done.2.first_ref
  21.3 1.7 collective-permute-done.3.second_ref
  23.0 29.4 %all-to-all-done = bf16[16,256,384]{2,1,0:T(8,128)(2,1)S(1)} async-done(((bf16[16,256,384]{2,1,0:T(8,128)(2,1)}), bf16[16,256,384]{2,1,0:T(8,128)(2,1)S(1)}, u32[]{:S(2)}, u32[]{:S(2)}) %all-to-all-start) | async-done | bytes 3145760 | tf_op jit(solution)/shard_map/all_to_all | solution.py:41
  53.2 2.9 %shard_map.77 = (f32[512,4096]{1,0:T(8,128)S(1)}, f32[256,256]{1,0:T(8,128)S(1)}, f32[256,256]{1,0:T(8,128)S(1)}) custom-call(bf16[256,128]{1,0:T(8,128)(2,1)S(1)} %collective-permute-done.2.first_ref, bf16[256,128]{1,0:T(8,128)(2,1)S(1)} %collective-permute-done.3.second_ref, bf16[4096,384]{1,0:T(8,128)(2,1)S(1)} %bitcast.37, f32[8,4096]{1,0:T(8,128)S(1)} %shard_map.76.norm_ref), custom_call_target="tpu_custom_call" | custom-call | tf_op jit(solution)/shard_map/pallas_call | solution.py:28
  56.1 3.1 %collective-permute-start.5 = (f32[256,256]{1,0:T(8,128)S(1)}, f32[256,256]{1,0:T(8,128)S(1)}, u32[]{:S(2)}, u32[]{:S(2)}) collective-permute-start(f32[256,256]{1,0:T(8,128)S(1)} %get-tuple-element.51), channel_id=1, source_target_pairs={{0,1},{1,0},{2,3},{3,2},{4,5},{5,4},{6,7},{7,6},{8,9},{9,8},{10,11... | collective-permute-start | bytes 786440 | tf_op jit(solution)/shard_map/ppermute | solution.py:437
  59.2 2.4 %collective-permute-start.6 = (bf16[256,128]{1,0:T(8,128)(2,1)S(1)}, bf16[256,128]{1,0:T(8,128)(2,1)S(1)}, u32[]{:S(2)}, u32[]{:S(2)}) collective-permute-start(bf16[256,128]{1,0:T(8,128)(2,1)S(1)} %get-tuple-element.57.first_ref), channel_id=1, source_target_pairs={{0,7},{1,6},{2,1},{3,0},{4,3},{5,2},{6,5},{7,4},{8,15},{9,14},{10,... | collective-permute-start | bytes 196616 | tf_op jit(solution)/shard_map/ppermute | solution.py:424
  61.6 2.9 %shard_map.78 = (f32[512,4096]{1,0:T(8,128)S(1)}, f32[256,256]{1,0:T(8,128)S(1)}, f32[256,256]{1,0:T(8,128)S(1)}) custom-call(bf16[256,128]{1,0:T(8,128)(2,1)S(1)} %collective-permute-done.first_ref, bf16[256,128]{1,0:T(8,128)(2,1)S(1)} %collective-permute-done.1.second_ref, bf16[4096,384]{1,0:T(8,128)(2,1)S(1)} %bitcast.38, f32[8,4096]{1,0:T(8,128)S(1)} %shard_map.76.norm_ref), custom_call_target="tpu_custom_call" | custom-call | tf_op jit(solution)/shard_map/pallas_call | solution.py:28
  65.2 2.9 %shard_map.79 = (f32[512,4096]{1,0:T(8,128)S(1)}, f32[256,256]{1,0:T(8,128)S(1)}, f32[256,256]{1,0:T(8,128)S(1)}) custom-call(bf16[256,128]{1,0:T(8,128)(2,1)S(1)} %collective-permute-done.4.first_ref, bf16[256,128]{1,0:T(8,128)(2,1)S(1)} %collective-permute-done.6.second_ref, bf16[4096,384]{1,0:T(8,128)(2,1)S(1)} %bitcast.39, f32[8,4096]{1,0:T(8,128)S(1)} %shard_map.76.norm_ref), custom_call_target="tpu_custom_call" | custom-call | tf_op jit(solution)/shard_map/pallas_call | solution.py:28
  68.7 1.1 collective-permute-done.8.second_ref
  69.8 2.9 %shard_map.80 = (f32[512,4096]{1,0:T(8,128)S(1)}, f32[256,256]{1,0:T(8,128)S(1)}, f32[256,256]{1,0:T(8,128)S(1)}) custom-call(bf16[256,128]{1,0:T(8,128)(2,1)S(1)} %get-tuple-element.57.first_ref, bf16[256,128]{1,0:T(8,128)(2,1)S(1)} %collective-permute-done.8.second_ref, bf16[4096,384]{1,0:T(8,128)(2,1)S(1)} %bitcast.40, f32[8,4096]{1,0:T(8,128)S(1)} %shard_map.76.norm_ref), custom_call_target="tpu_custom_call" | custom-call | tf_op jit(solution)/shard_map/pallas_call | solution.py:28
  72.9 1.4 collective-permute-start.11
  75.7 4.7 %collective-permute-done.11.two_ref = f32[256,256]{1,0:T(8,128)S(1)} collective-permute-done((f32[256,256]{1,0:T(8,128)S(1)}, f32[256,256]{1,0:T(8,128)S(1)}, u32[]{:S(2)}, u32[]{:S(2)}) %collective-permute-start.11) | collective-permute-done | bytes 262176 | tf_op jit(solution)/shard_map/ppermute | solution.py:441
  80.4 2.7 %collective-permute-done.10.one_ref = f32[256,256]{1,0:T(8,128)S(1)} collective-permute-done((f32[256,256]{1,0:T(8,128)S(1)}, f32[256,256]{1,0:T(8,128)S(1)}, u32[]{:S(2)}, u32[]{:S(2)}) %collective-permute-start.10) | collective-permute-done | bytes 262176 | tf_op jit(solution)/shard_map/ppermute | solution.py:441
  83.1 6.2 %collective-permute-done.13.three_ref = f32[256,256]{1,0:T(8,128)S(1)} collective-permute-done((f32[256,256]{1,0:T(8,128)S(1)}, f32[256,256]{1,0:T(8,128)S(1)}, u32[]{:S(2)}, u32[]{:S(2)}) %collective-permute-start.13) | collective-permute-done | bytes 262176 | tf_op jit(solution)/shard_map/ppermute | solution.py:441
  89.3 0.9 shard_map.81
  90.4 19.3 %all_to_all.76 = f32[128,1,512]{2,1,0:T(1,128)S(1)} all-to-all(f32[128,1,512]{2,1,0:T(1,128)S(1)} %copy.8), channel_id=1, replica_groups=mesh['row_0'=4,'row_1'=4,'col_0'=4,'col_1'=2] {'col_0','col_1','row_0','..., dimensions={0} | all-to-all | bytes 524288 | tf_op jit(solution)/shard_map/all_to_all | solution.py:41
  110.1 15.2 %all_to_all.77 = f32[128,1,512]{2,1,0:T(1,128)S(1)} all-to-all(f32[128,1,512]{2,1,0:T(1,128)S(1)} %copy.9), channel_id=1, replica_groups=mesh['row_0'=4,'row_1'=4,'col_0'=4,'col_1'=2] {'col_0','col_1','row_0','..., dimensions={0} | all-to-all | bytes 524288 | tf_op jit(solution)/shard_map/all_to_all | solution.py:41
  125.3 9.9 %shard_map.83 = (f32[256,256]{1,0:T(8,128)S(1)}, f32[8,256]{1,0:T(8,128)S(1)}, f32[16,256]{1,0:T(8,128)S(1)}) custom-call(f32[128,512]{1,0:T(8,128)S(1)} %bitcast.43, f32[256,256]{1,0:T(8,128)S(1)} %get-tuple-element.66.sketch_ref, f32[1,256]{1,0:T(1,128)S(1)} %bitcast.54, f32[1,1]{1,0:T(1,128)} %bitcast.32.ridge_ref), custom_call_target="tpu_custom_call" | custom-call | tf_op jit(solution)/shard_map/pallas_call | solution.py:28
  135.2 9.1 %all_to_all.78 = f32[16,1,256]{2,1,0:T(1,128)S(1)} all-to-all(f32[16,1,256]{2,1,0:T(1,128)S(1)} %copy.10), channel_id=1, replica_groups=mesh['row_0'=4,'row_1'=4,'col_0'=4,'col_1'=2] {'row_0','row_1'}, dimensions={0} | all-to-all | bytes 32768 | tf_op jit(solution)/shard_map/all_to_all | solution.py:41
  144.3 2.9 %shard_map.84 = f32[8,8,256]{2,1,0:T(8,128)S(1)} custom-call(f32[512,4096]{1,0:T(8,128)S(1)} %get-tuple-element.45.refs_0_, f32[512,4096]{1,0:T(8,128)S(1)} %get-tuple-element.48.refs_1_, f32[512,4096]{1,0:T(8,128)S(1)} %get-tuple-element.53.refs_2_, f32[512,4096]{1,0:T(8,128)S(1)} %get-tuple-element.58.refs_3_, f32[16,256]{1,0:T(8,128)S(1)} %bitcast.52), custom_call_target="tpu_custom_call" | custom-call | tf_op jit(solution)/shard_map/pallas_call | solution.py:28
  147.2 9.4 %all_to_all.79.parts_ref = f32[8,8,256]{2,1,0:T(8,128)S(1)} all-to-all(f32[8,8,256]{2,1,0:T(8,128)S(1)} %shard_map.84), channel_id=1, replica_groups=mesh['row_0'=4,'row_1'=4,'col_0'=4,'col_1'=2] {'col_0','col_1'}, dimensions={0} | all-to-all | bytes 131072 | tf_op jit(solution)/shard_map/all_to_all | solution.py:41
  157.1 14.5 %all_to_all.80 = f32[128,1,384]{2,1,0:T(1,128)S(1)} all-to-all(f32[128,1,384]{2,1,0:T(1,128)S(1)} %copy.11), channel_id=1, replica_groups=mesh['row_0'=4,'row_1'=4,'col_0'=4,'col_1'=2] {'col_0','col_1','row_0','..., dimensions={0} | all-to-all | bytes 393216 | tf_op jit(solution)/shard_map/all_to_all | solution.py:41
  172.5 14.2 %all_to_all.81 = f32[128,1,256]{2,1,0:T(1,128)S(1)} all-to-all(f32[128,1,256]{2,1,0:T(1,128)S(1)} %copy.12), channel_id=1, replica_groups=mesh['row_0'=4,'row_1'=4,'col_0'=4,'col_1'=2] {'col_0','col_1','row_0','..., dimensions={0} | all-to-all | bytes 262144 | tf_op jit(solution)/shard_map/all_to_all | solution.py:41
  186.7 2.9 %shard_map.87 = f32[128,384]{1,0:T(8,128)S(1)} custom-call(f32[512,4096]{1,0:T(8,128)S(1)} %get-tuple-element.45.refs_0_, f32[512,4096]{1,0:T(8,128)S(1)} %get-tuple-element.48.refs_1_, f32[512,4096]{1,0:T(8,128)S(1)} %get-tuple-element.53.refs_2_, f32[512,4096]{1,0:T(8,128)S(1)} %get-tuple-element.58.refs_3_, f32[128,256]{1,0:T(8,128)S(1)} %bitcast.41), custom_call_target="tpu_custom_call" | custom-call | tf_op jit(solution)/shard_map/pallas_call | solution.py:28
  189.8 14.6 %all_to_all.82 = f32[128,1,384]{2,1,0:T(1,128)S(1)} all-to-all(f32[128,1,384]{2,1,0:T(1,128)S(1)} %copy.13), channel_id=1, replica_groups=mesh['row_0'=4,'row_1'=4,'col_0'=4,'col_1'=2] {'col_0','col_1','row_0','..., dimensions={0} | all-to-all | bytes 393216 | tf_op jit(solution)/shard_map/all_to_all | solution.py:41
  (38 shorter events, 6.1 us)
Async XLA Ops:
  3.5 48.9 %all-to-all-start = ((bf16[16,256,384]{2,1,0:T(8,128)(2,1)}), bf16[16,256,384]{2,1,0:T(8,128)(2,1)S(1)}, u32[]{:S(2)}, u32[]{:S(2)}) async-start(bf16[16,256,384]{2,1,0:T(8,128)(2,1)} %get-tuple-element.40), calls=%async_computation | async-start | bytes 6291456 | tf_op jit(solution)/shard_map/all_to_all | solution.py:41
  12.1 7.5 %collective-permute-start = (bf16[256,128]{1,0:T(8,128)(2,1)S(1)}, bf16[256,128]{1,0:T(8,128)(2,1)S(1)}, u32[]{:S(2)}, u32[]{:S(2)}) collective-permute-start(bf16[256,128]{1,0:T(8,128)(2,1)S(1)} %get-tuple-element.57.first_ref), channel_id=1, source_target_pairs={{0,2},{1,3},{2,4},{3,5},{4,6},{5,7},{6,0},{7,1},{8,10},{9,11},{10,... | collective-permute-start | bytes 196616 | tf_op jit(solution)/shard_map/ppermute | solution.py:424
  13.3 6.2 %collective-permute-start.1 = (bf16[256,128]{1,0:T(8,128)(2,1)S(1)}, bf16[256,128]{1,0:T(8,128)(2,1)S(1)}, u32[]{:S(2)}, u32[]{:S(2)}) collective-permute-start(bf16[256,128]{1,0:T(8,128)(2,1)S(1)} %get-tuple-element.57.first_ref), channel_id=1, source_target_pairs={{0,3},{1,2},{2,5},{3,4},{4,7},{5,6},{6,1},{7,0},{8,11},{9,10},{10,... | collective-permute-start | bytes 196616 | tf_op jit(solution)/shard_map/ppermute | solution.py:424
  15.7 5.6 %collective-permute-start.2 = (bf16[256,128]{1,0:T(8,128)(2,1)S(1)}, bf16[256,128]{1,0:T(8,128)(2,1)S(1)}, u32[]{:S(2)}, u32[]{:S(2)}) collective-permute-start(bf16[256,128]{1,0:T(8,128)(2,1)S(1)} %get-tuple-element.57.first_ref), channel_id=1, source_target_pairs={{0,4},{1,5},{2,6},{3,7},{4,0},{5,1},{6,2},{7,3},{8,12},{9,13},{10,... | collective-permute-start | bytes 196616 | tf_op jit(solution)/shard_map/ppermute | solution.py:424
  17.1 5.9 %collective-permute-start.3 = (bf16[256,128]{1,0:T(8,128)(2,1)S(1)}, bf16[256,128]{1,0:T(8,128)(2,1)S(1)}, u32[]{:S(2)}, u32[]{:S(2)}) collective-permute-start(bf16[256,128]{1,0:T(8,128)(2,1)S(1)} %get-tuple-element.57.first_ref), channel_id=1, source_target_pairs={{0,5},{1,4},{2,7},{3,6},{4,1},{5,0},{6,3},{7,2},{8,13},{9,12},{10,... | collective-permute-start | bytes 196616 | tf_op jit(solution)/shard_map/ppermute | solution.py:424
  18.1 4.9 %collective-permute-start.4 = (bf16[256,128]{1,0:T(8,128)(2,1)S(1)}, bf16[256,128]{1,0:T(8,128)(2,1)S(1)}, u32[]{:S(2)}, u32[]{:S(2)}) collective-permute-start(bf16[256,128]{1,0:T(8,128)(2,1)S(1)} %get-tuple-element.57.first_ref), channel_id=1, source_target_pairs={{0,6},{1,7},{2,0},{3,1},{4,2},{5,3},{6,4},{7,5},{8,14},{9,15},{10,... | collective-permute-start | bytes 196616 | tf_op jit(solution)/shard_map/ppermute | solution.py:424
  53.2 36.1 %copy-start = (bf16[256,256]{1,0:T(8,128)(2,1)S(1)}, bf16[256,256]{1,0:T(8,128)(2,1)}, u32[]{:S(2)}) copy-start(bf16[256,256]{1,0:T(8,128)(2,1)} %test_ref.3) | copy-start | bytes 393220
  53.2 36.1 %copy-start.1 = (f32[256]{0:T(256)S(1)}, f32[256]{0:T(256)}, u32[]{:S(2)}) copy-start(f32[256]{0:T(256)} %param.8) | copy-start | bytes 3076
  56.1 9.1 %collective-permute-start.5 = (f32[256,256]{1,0:T(8,128)S(1)}, f32[256,256]{1,0:T(8,128)S(1)}, u32[]{:S(2)}, u32[]{:S(2)}) collective-permute-start(f32[256,256]{1,0:T(8,128)S(1)} %get-tuple-element.51), channel_id=1, source_target_pairs={{0,1},{1,0},{2,3},{3,2},{4,5},{5,4},{6,7},{7,6},{8,9},{9,8},{10,11... | collective-permute-start | bytes 786440 | tf_op jit(solution)/shard_map/ppermute | solution.py:437
  59.2 6.0 %collective-permute-start.6 = (bf16[256,128]{1,0:T(8,128)(2,1)S(1)}, bf16[256,128]{1,0:T(8,128)(2,1)S(1)}, u32[]{:S(2)}, u32[]{:S(2)}) collective-permute-start(bf16[256,128]{1,0:T(8,128)(2,1)S(1)} %get-tuple-element.57.first_ref), channel_id=1, source_target_pairs={{0,7},{1,6},{2,1},{3,0},{4,3},{5,2},{6,5},{7,4},{8,15},{9,14},{10,... | collective-permute-start | bytes 196616 | tf_op jit(solution)/shard_map/ppermute | solution.py:424
  64.5 4.2 %collective-permute-start.7 = (f32[256,256]{1,0:T(8,128)S(1)}, f32[256,256]{1,0:T(8,128)S(1)}, u32[]{:S(2)}, u32[]{:S(2)}) collective-permute-start(f32[256,256]{1,0:T(8,128)S(1)} %get-tuple-element.56), channel_id=1, source_target_pairs={{0,1},{1,0},{2,3},{3,2},{4,5},{5,4},{6,7},{7,6},{8,9},{9,8},{10,11... | collective-permute-start | bytes 786440 | tf_op jit(solution)/shard_map/ppermute | solution.py:437
  68.1 6.2 %collective-permute-start.12 = (f32[256,256]{1,0:T(8,128)S(1)}, f32[256,256]{1,0:T(8,128)S(1)}, u32[]{:S(2)}, u32[]{:S(2)}) collective-permute-start(f32[256,256]{1,0:T(8,128)S(1)} %get-tuple-element.64), channel_id=1, source_target_pairs={{0,1},{1,0},{2,3},{3,2},{4,5},{5,4},{6,7},{7,6},{8,9},{9,8},{10,11... | collective-permute-start | bytes 786440 | tf_op jit(solution)/shard_map/ppermute | solution.py:437
  68.3 1.5 collective-permute-start.8
  72.7 3.0 %collective-permute-start.9 = (f32[256,256]{1,0:T(8,128)S(1)}, f32[256,256]{1,0:T(8,128)S(1)}, u32[]{:S(2)}, u32[]{:S(2)}) collective-permute-start(f32[256,256]{1,0:T(8,128)S(1)} %get-tuple-element.60), channel_id=1, source_target_pairs={{0,1},{1,0},{2,3},{3,2},{4,5},{5,4},{6,7},{7,6},{8,9},{9,8},{10,11... | collective-permute-start | bytes 786440 | tf_op jit(solution)/shard_map/ppermute | solution.py:437
  72.9 7.5 %collective-permute-start.11 = (f32[256,256]{1,0:T(8,128)S(1)}, f32[256,256]{1,0:T(8,128)S(1)}, u32[]{:S(2)}, u32[]{:S(2)}) collective-permute-start(f32[256,256]{1,0:T(8,128)S(1)} %add.10), channel_id=1, source_target_pairs={{0,6},{2,0},{4,2},{6,4},{1,7},{3,1},{5,3},{7,5},{8,14},{10,8},{12,... | collective-permute-start | bytes 786440 | tf_op jit(solution)/shard_map/ppermute | solution.py:441
  74.3 8.8 %collective-permute-start.10 = (f32[256,256]{1,0:T(8,128)S(1)}, f32[256,256]{1,0:T(8,128)S(1)}, u32[]{:S(2)}, u32[]{:S(2)}) collective-permute-start(f32[256,256]{1,0:T(8,128)S(1)} %add.9), channel_id=1, source_target_pairs={{0,4},{2,6},{4,0},{6,2},{1,5},{3,7},{5,1},{7,3},{8,12},{10,14},{12... | collective-permute-start | bytes 786440 | tf_op jit(solution)/shard_map/ppermute | solution.py:441
  74.3 14.9 %collective-permute-start.13 = (f32[256,256]{1,0:T(8,128)S(1)}, f32[256,256]{1,0:T(8,128)S(1)}, u32[]{:S(2)}, u32[]{:S(2)}) collective-permute-start(f32[256,256]{1,0:T(8,128)S(1)} %add.11), channel_id=1, source_target_pairs={{0,2},{2,4},{4,6},{6,0},{1,3},{3,5},{5,7},{7,1},{8,10},{10,12},{12... | collective-permute-start | bytes 786440 | tf_op jit(solution)/shard_map/ppermute | solution.py:441

commit v2 on v1

--- a/solution.py
+++ b/solution.py
@@ -9,9 +9,11 @@
 from jax.sharding import PartitionSpec as P
 
 
-ROW = ("row_0", "row_1")
-COL = ("col_0", "col_1")
-COL_ROW = ("col_0", "col_1", "row_0", "row_1")
+AXES = ("row_0", "row_1", "row_2", "col_0", "col_1")
+ALL = ("col_0", "col_1", "row_0", "row_1", "row_2")
+NEAR_COLUMNS = ("row_0", "row_2")
+COLUMNS = ("col_1", "row_0", "row_2")
+ROWS = ("row_1", "col_0")
 LOG2E = 1.4426950408889634
 MIB = 1024 * 1024
 F32 = jnp.float32
@@ -19,7 +21,6 @@
 HIGH = lax.Precision.HIGHEST
 KERN_SPACE = pltpu.VMEM
 ORDER = (2, 1, 3, 0)
-LATE = ((0, 1), (3, 1))
 KLIMIT = 4
 KLIMIT2 = 4
 
@@ -115,13 +116,18 @@
         norm_ref[:, base : base + 128] = eight(jnp.sum(packed, axis=0, keepdims=True))
 
 
-def block_body(first_ref, second_ref, message_ref, norm_ref, kern_ref, own_ref, other_ref, *, chunk):
+def block_body(*refs, chunk, has_before):
+    first_ref, second_ref, message_ref, norm_ref, *rest = refs
     parts = jnp.concatenate([first_ref[...], second_ref[...]], axis=0)
     turned = pltpu.roll(parts.astype(F32), 64, 1)
     points = parts.astype(F32) + turned
     left_norm = -0.25 * jnp.sum(points * points, axis=1, keepdims=True)
     left = jnp.concatenate([parts, turned.astype(BF16)], axis=1)
     total = None
+    if has_before:
+        own_before_ref, other_before_ref, *rest = rest
+        total = jnp.concatenate([own_before_ref[...], other_before_ref[...]], axis=0)
+    kern_ref, own_ref, other_ref = rest
     for start in range(0, message_ref.shape[0], chunk):
         span = slice(start, start + chunk)
         right = message_ref[span, 0:128]
@@ -142,23 +148,27 @@
     other_ref[...] = total[half:]
 
 
-def kernel_block(first, second, message, norm):
+def kernel_block(first, second, message, norm, before=()):
     rows, columns, rank = first.shape[0], message.shape[0], message.shape[1] - 128
     return call(
-        functools.partial(block_body, chunk=512),
+        functools.partial(block_body, chunk=512, has_before=bool(before)),
         [KERN_SPACE((2 * rows, columns), F32), shape(rows, rank), shape(rows, rank)],
         first,
         second,
         message,
         norm,
+        *before,
         limit=KLIMIT,
     )
 
 
 def core_body(
-    near_ref, swapped_ref, one_ref, two_ref, three_ref, test_ref, targets_ref, ridge_ref, sketch_ref, copy_ref, out_ref
+    *refs
 ):
-    sketch = near_ref[...] + swapped_ref[...] + one_ref[...] + two_ref[...] + three_ref[...]
+    *part_refs, test_ref, targets_ref, ridge_ref, sketch_ref, copy_ref, out_ref = refs
+    sketch = part_refs[0][...]
+    for part_ref in part_refs[1:]:
+        sketch = sketch + part_ref[...]
     sketch_ref[...] = sketch
     copy_ref[...] = sketch
     shifted = ridge_ref[0, 0] * test_ref[...].astype(F32) + sketch
@@ -283,54 +293,83 @@
 
 
 def products(kern_refs, vector):
-    tiles = kern_refs[0].shape[1] // 128
     sub = lax.broadcasted_iota(jnp.int32, (8, 128), 0)
     lane = lax.broadcasted_iota(jnp.int32, (8, 128), 1)
-    chip, core = lax.axis_index("col_0"), lax.axis_index("col_1")
-    chips = len(kern_refs)
-    for shift, kern_ref in zip(ORDER, kern_refs):
-        for flip in range(2):
-            place = (chip + (chips - shift)) % chips * 2 + (core + flip) % 2
-            for half in range(2):
+    chips = len(ORDER)
+    tiles = kern_refs[0].shape[1] // 128
+    for number, shift in enumerate(ORDER):
+        pair = (kern_refs[number], kern_refs[number + chips])
+        for half in range(2):
+            pieces = []
+            for flip in range(2):
                 packed = jnp.zeros((8, 128), F32)
                 for start in range(0, 128, 64):
                     base = flip * 256 + half * 128 + start
                     acc = [None] * 8
-                    for k in range(tiles):
+                    for k in range(2 * tiles):
                         span = slice(k % 2 * 128, k % 2 * 128 + 128)
                         piece = eight(vector[k // 2 : k // 2 + 1, span])
+                        at = k % tiles * 128
                         for g in range(8):
-                            block = kern_ref[
-                                base + g * 8 : base + g * 8 + 8, k * 128 : k * 128 + 128
+                            block = pair[k // tiles][
+                                base + g * 8 : base + g * 8 + 8, at : at + 128
                             ]
                             acc[g] = block * piece if k == 0 else acc[g] + block * piece
                     for g in range(8):
                         total = jnp.sum(acc[g], axis=1, keepdims=True)
                         packed = packed + jnp.where(lane == sub + (start + g * 8), total, 0.0)
-                yield place, half, jnp.sum(packed, axis=0, keepdims=True)
+                pieces.append(jnp.sum(packed, axis=0, keepdims=True))
+            yield shift, half, pieces
+
+
+def own_first(lower, upper):
+    core = lax.axis_index("col_1")
+    return jnp.concatenate(
+        [jnp.where(core == 0, lower, upper), jnp.where(core == 0, upper, lower)], axis=0
+    )
+
+
+def owner(shift):
+    chips = len(ORDER)
+    return (lax.axis_index("col_0") + (chips - shift)) % chips
 
 
 def product_body(*refs):
     *kern_refs, vector_ref, out_ref = refs
-    for place, half, piece in products(kern_refs, vector_ref):
-        out_ref[place, :, half * 128 : half * 128 + 128] = eight(piece)
+    half_y = lax.axis_index("row_1")
+    chips = len(ORDER)
+    vector = own_first(vector_ref[0:8, :], vector_ref[8:16, :])
+    for shift, half, pieces in products(kern_refs, vector):
+        span = slice(half * 128, half * 128 + 128)
+        out_ref[half_y * chips + owner(shift), :, span] = eight(pieces[0])
+        out_ref[(1 - half_y) * chips + owner(shift), :, span] = eight(pieces[1])
 
 
 def last_product_body(*refs):
     *kern_refs, vector_ref, out_ref = refs
-    rows = out_ref.shape[0] // 8
-    own_place = lax.axis_index("col_0") * 2 + lax.axis_index("col_1")
-    own_row = lax.axis_index("row_0") * 4 + lax.axis_index("row_1")
-    mine = lax.broadcasted_iota(jnp.int32, (rows, 128), 0) == own_row
-    curve = jnp.zeros((rows, 128), F32)
-
-    def group(place):
-        return pl.ds(pl.multiple_of(place * rows, rows), rows)
-
-    for place, half, piece in products(kern_refs, vector_ref[group(own_place), :]):
+    chip, core = lax.axis_index("col_0"), lax.axis_index("col_1")
+    far_y, half_y, z = lax.axis_index("row_0"), lax.axis_index("row_1"), lax.axis_index("row_2")
+
+    def group(chip, core, far_y):
+        return pl.ds(pl.multiple_of(chip * 32 + core * 16 + far_y * 8, 8), 8)
+
+    def columns_of(core):
+        rows = [vector_ref[group(chip, core, far), :] for far in range(2)]
+        return jnp.concatenate(
+            [jnp.where(half_y == 0, block[0:4], block[4:8]) for block in rows], axis=0
+        )
+
+    sub = lax.broadcasted_iota(jnp.int32, (8, 128), 0)
+    mine = sub // 4 == half_y
+    curve = jnp.zeros((8, 128), F32)
+    out_ref[...] = jnp.zeros(out_ref.shape, F32)
+    vector = own_first(columns_of(0), columns_of(1))
+    for shift, half, pieces in products(kern_refs, vector):
         span = slice(half * 128, half * 128 + 128)
-        curve = curve + piece * jnp.where(mine, vector_ref[group(place), span], 0.0)
-        out_ref[group(place), span] = jnp.broadcast_to(piece, (rows, 128))
+        rows = group(owner(shift), core, far_y)
+        both = jnp.where(mine, pieces[0], pieces[1])
+        out_ref[rows, span] = both
+        curve = curve + jnp.where(sub % 4 == z, both * vector_ref[rows, span], 0.0)
     curve = jnp.sum(curve, axis=0, keepdims=True)
     out_ref[:, 256:384] = jnp.broadcast_to(curve, (out_ref.shape[0], 128))
 
@@ -389,10 +428,10 @@
     residual_ref,
 ):
     ridge = ridge_ref[0, 0]
-    own_row = lax.axis_index("row_0") * 4 + lax.axis_index("row_1")
-    rows = parts_ref.shape[0] // 8
+    group = lax.axis_index("col_1") * 2 + lax.axis_index("row_0")
     direction = next_ref[0:1, :]
-    mine = lax.broadcasted_iota(jnp.int32, (8 * rows, 256), 0) % rows == own_row
+    row = lax.broadcasted_iota(jnp.int32, (parts_ref.shape[0], 256), 0)
+    mine = (row % 32 // 8 == group) & (row % 4 == lax.axis_index("row_2"))
     last = jnp.sum(jnp.where(mine, parts_ref[:, 0:256], 0.0), axis=0, keepdims=True)
     last = last + ridge * direction
     every = every_ref[...]
@@ -407,39 +446,41 @@
 
 
 def local(points, feature_scale, test_matrix, targets, ridge):
-    everyone = lax.axis_size(COL_ROW)
-    row_devices = lax.axis_size(ROW)
+    everyone = lax.axis_size(ALL)
+    column_devices, near_devices = lax.axis_size(COLUMNS), lax.axis_size(NEAR_COLUMNS)
     own, rank = test_matrix.shape
     ridge = ridge.reshape(1, 1)
     targets = targets.reshape(1, own)
     scale = feature_scale.reshape(1, -1)
-    parts, copies = parts_and_copies(points, scale, test_matrix, row_devices)
-    chips, cores = lax.axis_size("col_0"), lax.axis_size("col_1")
-    chunks = {}
-    for shift in range(chips):
-        for flip in range(cores):
-            pairs = [
-                (c, (c // 2 + shift) % chips * 2 + (c % 2 ^ flip)) for c in range(chips * cores)
-            ]
-            chunks[shift, flip] = lax.ppermute(parts, COL, pairs) if shift or flip else parts
-    message = exchanged(copies, ROW).reshape(-1, 128 + rank)
-    early = {key: value for key, value in chunks.items() if key not in LATE}
-    message, early = lax.optimization_barrier((message, early))
-    chunks.update(early)
+    parts, copies = parts_and_copies(points, scale, test_matrix, near_devices)
+    chips = lax.axis_size("col_0")
+
+    def along_rows(value, shift, flip):
+        pairs = [
+            (i, (i // chips ^ flip) * chips + (i + shift) % chips) for i in range(2 * chips)
+        ]
+        return lax.ppermute(value, ROWS, pairs) if shift or flip else value
+
+    chunks = {
+        (shift, flip): along_rows(parts, shift, flip) for shift in ORDER for flip in (0, 1)
+    }
+    message = exchanged(copies, NEAR_COLUMNS).reshape(-1, 128 + rank)
+    message, chunks = lax.optimization_barrier((message, chunks))
+    partner = lax.ppermute(message, "col_1", [(0, 1), (1, 0)])
     norm = call(norms_body, shape(8, message.shape[0]), message)
-    kerns, partial, sent = [], [], []
+    kerns, before, sums = [], [], []
+    for shift in ORDER:
+        kern, *sketches = kernel_block(chunks[shift, 0], chunks[shift, 1], message, norm)
+        kerns.append(kern)
+        before.append(sketches)
+    norm = call(norms_body, shape(8, message.shape[0]), partner)
     for number, shift in enumerate(ORDER):
-        first = chunks[shift, 0]
-        if number > 1:
-            first, partial[number - 2] = lax.optimization_barrier((first, partial[number - 2]))
-        kern, near, other = kernel_block(first, chunks[shift, 1], message, norm)
+        kern, *sketches = kernel_block(
+            chunks[shift, 0], chunks[shift, 1], partner, norm, before[number]
+        )
         kerns.append(kern)
-        swapped = lax.ppermute(other, "col_1", [(0, 1), (1, 0)])
-        partial.append(near + swapped if shift else (near, swapped))
-    for number, shift in enumerate(ORDER[:-1]):
-        pairs = [(c, (c - shift) % chips) for c in range(chips)]
-        sent.append(lax.ppermute(partial[number], "col_0", pairs))
-    sums = [*partial[-1], *sent]
+        for flip in (1, 0):
+            sums.append(along_rows(sketches[flip], -shift, flip))
     sketch_out, sketch, packed = call(
         core_body,
         [shape(own, rank), shape(own, rank), shape(everyone, 512)],
@@ -448,22 +489,22 @@
         targets,
         ridge,
     )
-    packed = exchanged(packed, COL_ROW)
+    packed = exchanged(packed, ALL)
     packed = call(summed_body, shape(everyone, 512), packed)
-    packed = exchanged(packed, COL_ROW)
+    packed = exchanged(packed, ALL)
     inverse, state, send = call(
         first_body,
-        [shape(rank, rank), shape(8, own), shape(row_devices, own)],
+        [shape(rank, rank), shape(8, own), shape(column_devices, own)],
         packed,
         sketch,
         targets,
         ridge,
     )
-    product = kernel_times(kerns, exchanged(send, ROW))
+    product = kernel_times(kerns, exchanged(send, COLUMNS))
     image, send = call(
         image_body,
         [shape(8, own), shape(everyone, 384)],
-        exchanged(product, COL),
+        exchanged(product, ROWS),
         state,
         sketch,
         targets,
@@ -472,7 +513,7 @@
     following, send = call(
         second_body,
         [shape(8, own), shape(everyone, own)],
-        exchanged(send, COL_ROW),
+        exchanged(send, ALL),
         state,
         image,
         inverse,
@@ -480,12 +521,12 @@
         targets,
         ridge,
     )
-    every = exchanged(send, COL_ROW)
+    every = exchanged(send, ALL)
     product = call(last_product_body, shape(everyone, 384), *kerns, every, limit=KLIMIT2)
     coefficients, residual = call(
         finish_body,
         [shape(1, own), shape(1, own)],
-        exchanged(product, COL_ROW),
+        exchanged(product, ALL),
         every,
         state,
         following,
@@ -497,12 +538,12 @@
 
 
 def solution(mesh):
-    split = Mesh(mesh.devices.reshape(4, 4, 4, 2), ROW + COL)
+    split = Mesh(mesh.devices.reshape(2, 2, 4, 4, 2), AXES)
 
     return jax.shard_map(
         local,
         mesh=split,
-        in_specs=(P(COL_ROW, None), P(), P(COL_ROW, None), P(COL_ROW), P()),
-        out_specs=(P(COL_ROW), P(COL_ROW), P(COL_ROW, None)),
+        in_specs=(P(ALL, None), P(), P(ALL, None), P(ALL), P()),
+        out_specs=(P(ALL), P(ALL), P(ALL, None)),
         check_vma=False,
     )

time: 205 us -> 197 us (0.961)
  waiting for transfers between devices: 47.5 us -> 32.5 us
  starting transfers between devices: 25.2 us -> 30.5 us
    all_to_all x1, waiting for transfers between devices: 29.4 us -> 0.01 us  [exchanged(): return lax.all_to_all(pieces, axes, 0, 0, tiled=True)]
    ppermute x14 -> x15, waiting for transfers between devices: 18.1 us -> 32.5 us  [the longest x14 31.7 us: along_rows(): return lax.ppermute(value, ROWS, pairs) if shift or flip else value]
    ppermute x14 -> x15, starting transfers between devices: 16.6 us -> 22 us  [the longest x14 19.1 us: along_rows(): return lax.ppermute(value, ROWS, pairs) if shift or flip else value]
    pallas_call x13 -> x18, Pallas kernels: 30.5 us -> 30.8 us  [call(): pl.pallas_call(body, out_shape=outs, scratch_shapes=list(scratch), compil...]
  transfers between devices with their start and end apart: 15 -> 16, of which waited for: 7 -> 7; matrix products, arithmetic and copies ran while one was open for 0% -> 0% of each run, Pallas kernels for 4% -> 6%
where the time goes in v2:
time: 197 us; the launch traced here: 196 us
  blocking collectives  97.5 us (49%)
  Pallas kernels  33.1 us (17%)
  waiting for transfers between devices  32.5 us (16%)
  starting transfers between devices  30.5 us (15%)
    all_to_all x7, blocking collectives, exchanged(): return lax.all_to_all(pieces, axes, 0, 0, tiled=True)  97.5 us
    ppermute x14, waiting for transfers between devices, along_rows(): return lax.ppermute(value, ROWS, pairs) if shift or flip else value  31.7 us
    pallas_call x18, Pallas kernels, call(): pl.pallas_call(body, out_shape=outs, scratch_shapes=list(scratch), compil...  30.8 us
    ppermute x14, starting transfers between devices, along_rows(): return lax.ppermute(value, ROWS, pairs) if shift or flip else value  19.1 us
    all_to_all x1, starting transfers between devices, exchanged(): return lax.all_to_all(pieces, axes, 0, 0, tiled=True)  8.49 us
  transfers between devices with their start and end apart: 16, of which 7 were waited for; matrix products, arithmetic and copies ran while one was open for 0% of the time, Pallas kernels for 6%

profile of v2, /device:TPU:1, one launch (start us, length us, event | category | flops | bytes accessed | tf_op | source)
XLA Modules:
  0.0 196.4 jit_solution(15307830838418797400)
XLA Ops:
  0.6 2.3 %parts.1 = (bf16[256,128]{1,0:T(8,128)(2,1)S(1)}, bf16[8,256,384]{2,1,0:T(8,128)(2,1)}) custom-call(f32[64,256]{1,0:T(8,128)} %bitcast.60, f32[1,64]{1,0:T(1,128)} %bitcast.61, bf16[256,256]{1,0:T(8,128)(2,1)} %refs_8_.1), custom_call_target="tpu_custom_call" | custom-call | tf_op jit(solution)/shard_map/parts/pallas_call | solution.py:87
  2.9 8.5 %all-to-all-start = ((bf16[8,256,384]{2,1,0:T(8,128)(2,1)}), bf16[8,256,384]{2,1,0:T(8,128)(2,1)S(1)}, u32[]{:S(2)}, u32[]{:S(2)}) async-start(bf16[8,256,384]{2,1,0:T(8,128)(2,1)} %get-tuple-element.50), calls=%async_computation | async-start | bytes 3145728 | tf_op jit(solution)/shard_map/all_to_all | solution.py:42
  13.0 2.0 %collective-permute-start.2 = (bf16[256,128]{1,0:T(8,128)(2,1)S(1)}, bf16[256,128]{1,0:T(8,128)(2,1)S(1)}, u32[]{:S(2)}, u32[]{:S(2)}) collective-permute-start(bf16[256,128]{1,0:T(8,128)(2,1)S(1)} %get-tuple-element.62.refs_0_), channel_id=1, source_target_pairs={{0,34},{2,36},{4,38},{6,32},{32,2},{34,4},{36,6},{38,0},{1,35},{3,... | collective-permute-start | bytes 196616 | tf_op jit(solution)/shard_map/ppermute | solution.py:462
  15.0 1.4 collective-permute-start.3
  16.5 1.6 collective-permute-start.4
  18.1 15.1 %collective-permute-done.refs_1_ = bf16[256,128]{1,0:T(8,128)(2,1)S(1)} collective-permute-done((bf16[256,128]{1,0:T(8,128)(2,1)S(1)}, bf16[256,128]{1,0:T(8,128)(2,1)S(1)}, u32[]{:S(2)}, u32[]{:S(2)}) %collective-permute-start) | collective-permute-done | bytes 65568 | tf_op jit(solution)/shard_map/ppermute | solution.py:462
  33.2 2.5 %collective-permute-start.5 = (bf16[256,128]{1,0:T(8,128)(2,1)S(1)}, bf16[256,128]{1,0:T(8,128)(2,1)S(1)}, u32[]{:S(2)}, u32[]{:S(2)}) collective-permute-start(bf16[256,128]{1,0:T(8,128)(2,1)S(1)} %get-tuple-element.62.refs_0_), channel_id=1, source_target_pairs={{0,6},{2,0},{4,2},{6,4},{32,38},{34,32},{36,34},{38,36},{1,7},{3,1... | collective-permute-start | bytes 196616 | tf_op jit(solution)/shard_map/ppermute | solution.py:462
  37.1 2.8 %collective-permute-done.6.refs_1_ = bf16[256,128]{1,0:T(8,128)(2,1)S(1)} collective-permute-done((bf16[256,128]{1,0:T(8,128)(2,1)S(1)}, bf16[256,128]{1,0:T(8,128)(2,1)S(1)}, u32[]{:S(2)}, u32[]{:S(2)}) %collective-permute-start.6) | collective-permute-done | bytes 65568 | tf_op jit(solution)/shard_map/ppermute | solution.py:462
  39.8 2.9 %collective-permute-start.7 = (bf16[2048,384]{1,0:T(8,128)(2,1)S(1)}, bf16[2048,384]{1,0:T(8,128)(2,1)S(1)}, u32[]{:S(2)}, u32[]{:S(2)}) collective-permute-start(bf16[2048,384]{1,0:T(8,128)(2,1)S(1)} %bitcast.36), channel_id=1, source_target_pairs={{0,1},{1,0},{2,3},{3,2},{4,5},{5,4},{6,7},{7,6},{8,9},{9,8},{10,11... | collective-permute-start | bytes 4718600 | tf_op jit(solution)/shard_map/ppermute | solution.py:469
  43.2 1.7 shard_map.77
  46.2 1.4 shard_map.82
  49.0 2.5 %collective-permute-start.9 = (f32[256,256]{1,0:T(8,128)S(1)}, f32[256,256]{1,0:T(8,128)S(1)}, u32[]{:S(2)}, u32[]{:S(2)}) collective-permute-start(f32[256,256]{1,0:T(8,128)S(1)} %get-tuple-element.78), channel_id=1, source_target_pairs={{0,4},{2,6},{4,0},{6,2},{32,36},{34,38},{36,32},{38,34},{1,5},{3,7... | collective-permute-start | bytes 786440 | tf_op jit(solution)/shard_map/ppermute | solution.py:462
  51.5 1.7 shard_map.78
  53.2 1.7 shard_map.79
  54.9 1.7 shard_map.80
  56.6 1.4 shard_map.83
  58.0 1.9 collective-permute-start.10
  61.4 2.3 %collective-permute-start.12 = (f32[256,256]{1,0:T(8,128)S(1)}, f32[256,256]{1,0:T(8,128)S(1)}, u32[]{:S(2)}, u32[]{:S(2)}) collective-permute-start(f32[256,256]{1,0:T(8,128)S(1)} %get-tuple-element.81), channel_id=1, source_target_pairs={{0,34},{2,36},{4,38},{6,32},{32,2},{34,4},{36,6},{38,0},{1,35},{3,... | collective-permute-start | bytes 786440 | tf_op jit(solution)/shard_map/ppermute | solution.py:462
  66.3 4.2 %collective-permute-done.10.refs_2_ = f32[256,256]{1,0:T(8,128)S(1)} collective-permute-done((f32[256,256]{1,0:T(8,128)S(1)}, f32[256,256]{1,0:T(8,128)S(1)}, u32[]{:S(2)}, u32[]{:S(2)}) %collective-permute-start.10) | collective-permute-done | bytes 262176 | tf_op jit(solution)/shard_map/ppermute | solution.py:462
  70.6 5.0 %collective-permute-done.11.refs_3_ = f32[256,256]{1,0:T(8,128)S(1)} collective-permute-done((f32[256,256]{1,0:T(8,128)S(1)}, f32[256,256]{1,0:T(8,128)S(1)}, u32[]{:S(2)}, u32[]{:S(2)}) %collective-permute-start.11) | collective-permute-done | bytes 262176 | tf_op jit(solution)/shard_map/ppermute | solution.py:462
  75.6 1.6 collective-permute-done.13.refs_5_
  77.1 3.1 %collective-permute-done.14.refs_6_ = f32[256,256]{1,0:T(8,128)S(1)} collective-permute-done((f32[256,256]{1,0:T(8,128)S(1)}, f32[256,256]{1,0:T(8,128)S(1)}, u32[]{:S(2)}, u32[]{:S(2)}) %collective-permute-start.14) | collective-permute-done | bytes 262176 | tf_op jit(solution)/shard_map/ppermute | solution.py:462
  81.4 19.6 %all_to_all.76 = f32[128,1,512]{2,1,0:T(1,128)S(1)} all-to-all(f32[128,1,512]{2,1,0:T(1,128)S(1)} %copy.8), channel_id=1, replica_groups=mesh['row_0'=2,'row_1'=2,'row_2'=4,'col_0'=4,'col_1'=2] {'col_0','col_1'..., dimensions={0} | all-to-all | bytes 524288 | tf_op jit(solution)/shard_map/all_to_all | solution.py:42
  101.3 15.2 %all_to_all.77 = f32[128,1,512]{2,1,0:T(1,128)S(1)} all-to-all(f32[128,1,512]{2,1,0:T(1,128)S(1)} %copy.9), channel_id=1, replica_groups=mesh['row_0'=2,'row_1'=2,'row_2'=4,'col_0'=4,'col_1'=2] {'col_0','col_1'..., dimensions={0} | all-to-all | bytes 524288 | tf_op jit(solution)/shard_map/all_to_all | solution.py:42
  116.5 9.7 %shard_map.88 = (f32[256,256]{1,0:T(8,128)S(1)}, f32[8,256]{1,0:T(8,128)S(1)}, f32[16,256]{1,0:T(8,128)S(1)}) custom-call(f32[128,512]{1,0:T(8,128)S(1)} %bitcast.44, f32[256,256]{1,0:T(8,128)S(1)} %get-tuple-element.86.sketch_ref, f32[1,256]{1,0:T(1,128)S(1)} %bitcast.55, f32[1,1]{1,0:T(1,128)} %bitcast.32.ridge_ref), custom_call_target="tpu_custom_call" | custom-call | tf_op jit(solution)/shard_map/pallas_call | solution.py:29
  126.3 10.6 %all_to_all.78 = f32[16,1,256]{2,1,0:T(1,128)S(1)} all-to-all(f32[16,1,256]{2,1,0:T(1,128)S(1)} %copy.10), channel_id=1, replica_groups=mesh['row_0'=2,'row_1'=2,'row_2'=4,'col_0'=4,'col_1'=2] {'col_1','row_0'..., dimensions={0} | all-to-all | bytes 32768 | tf_op jit(solution)/shard_map/all_to_all | solution.py:42
  137.0 2.4 %shard_map.89 = f32[8,8,256]{2,1,0:T(8,128)S(1)} custom-call(f32[512,2048]{1,0:T(8,128)S(1)} %get-tuple-element.55.refs_0_, f32[512,2048]{1,0:T(8,128)S(1)} %get-tuple-element.58.refs_1_, f32[512,2048]{1,0:T(8,128)S(1)} %get-tuple-element.61.refs_2_, f32[512,2048]{1,0:T(8,128)S(1)} %get-tuple-element.64.refs_3_, f32[512,2048]{1,0:T(8,128)S(1)} %get-tuple-element.67.refs_4_, ...), custom_call_target="tpu_custom_call" | custom-call | tf_op jit(solution)/shard_map/pallas_call | solution.py:29
  139.4 7.7 %all_to_all.79.parts_ref = f32[8,8,256]{2,1,0:T(8,128)S(1)} all-to-all(f32[8,8,256]{2,1,0:T(8,128)S(1)} %shard_map.89), channel_id=1, replica_groups=mesh['row_0'=2,'row_1'=2,'row_2'=4,'col_0'=4,'col_1'=2] {'row_1','col_0'}, dimensions={0} | all-to-all | bytes 131072 | tf_op jit(solution)/shard_map/all_to_all | solution.py:42
  147.6 15.6 %all_to_all.80 = f32[128,1,384]{2,1,0:T(1,128)S(1)} all-to-all(f32[128,1,384]{2,1,0:T(1,128)S(1)} %copy.11), channel_id=1, replica_groups=mesh['row_0'=2,'row_1'=2,'row_2'=4,'col_0'=4,'col_1'=2] {'col_0','col_1'..., dimensions={0} | all-to-all | bytes 393216 | tf_op jit(solution)/shard_map/all_to_all | solution.py:42
  164.1 14.2 %all_to_all.81 = f32[128,1,256]{2,1,0:T(1,128)S(1)} all-to-all(f32[128,1,256]{2,1,0:T(1,128)S(1)} %copy.12), channel_id=1, replica_groups=mesh['row_0'=2,'row_1'=2,'row_2'=4,'col_0'=4,'col_1'=2] {'col_0','col_1'..., dimensions={0} | all-to-all | bytes 262144 | tf_op jit(solution)/shard_map/all_to_all | solution.py:42
  178.3 2.6 %shard_map.92 = f32[128,384]{1,0:T(8,128)S(1)} custom-call(f32[512,2048]{1,0:T(8,128)S(1)} %get-tuple-element.55.refs_0_, f32[512,2048]{1,0:T(8,128)S(1)} %get-tuple-element.58.refs_1_, f32[512,2048]{1,0:T(8,128)S(1)} %get-tuple-element.61.refs_2_, f32[512,2048]{1,0:T(8,128)S(1)} %get-tuple-element.64.refs_3_, f32[512,2048]{1,0:T(8,128)S(1)} %get-tuple-element.67.refs_4_, ...), custom_call_target="tpu_custom_call" | custom-call | tf_op jit(solution)/shard_map/pallas_call | solution.py:29
  181.1 14.6 %all_to_all.82 = f32[128,1,384]{2,1,0:T(1,128)S(1)} all-to-all(f32[128,1,384]{2,1,0:T(1,128)S(1)} %copy.13), channel_id=1, replica_groups=mesh['row_0'=2,'row_1'=2,'row_2'=4,'col_0'=4,'col_1'=2] {'col_0','col_1'..., dimensions={0} | all-to-all | bytes 393216 | tf_op jit(solution)/shard_map/all_to_all | solution.py:42
  (42 shorter events, 13.4 us)
Async XLA Ops:
  2.9 36.9 %all-to-all-start = ((bf16[8,256,384]{2,1,0:T(8,128)(2,1)}), bf16[8,256,384]{2,1,0:T(8,128)(2,1)S(1)}, u32[]{:S(2)}, u32[]{:S(2)}) async-start(bf16[8,256,384]{2,1,0:T(8,128)(2,1)} %get-tuple-element.50), calls=%async_computation | async-start | bytes 3145728 | tf_op jit(solution)/shard_map/all_to_all | solution.py:42
  11.4 21.8 %collective-permute-start = (bf16[256,128]{1,0:T(8,128)(2,1)S(1)}, bf16[256,128]{1,0:T(8,128)(2,1)S(1)}, u32[]{:S(2)}, u32[]{:S(2)}) collective-permute-start(bf16[256,128]{1,0:T(8,128)(2,1)S(1)} %get-tuple-element.62.refs_0_), channel_id=1, source_target_pairs={{0,32},{2,34},{4,36},{6,38},{32,0},{34,2},{36,4},{38,6},{1,33},{3,... | collective-permute-start | bytes 196616 | tf_op jit(solution)/shard_map/ppermute | solution.py:462
  11.8 23.9 %collective-permute-start.1 = (bf16[256,128]{1,0:T(8,128)(2,1)S(1)}, bf16[256,128]{1,0:T(8,128)(2,1)S(1)}, u32[]{:S(2)}, u32[]{:S(2)}) collective-permute-start(bf16[256,128]{1,0:T(8,128)(2,1)S(1)} %get-tuple-element.62.refs_0_), channel_id=1, source_target_pairs={{0,2},{2,4},{4,6},{6,0},{32,34},{34,36},{36,38},{38,32},{1,3},{3,5... | collective-permute-start | bytes 196616 | tf_op jit(solution)/shard_map/ppermute | solution.py:462
  13.0 24.0 %collective-permute-start.2 = (bf16[256,128]{1,0:T(8,128)(2,1)S(1)}, bf16[256,128]{1,0:T(8,128)(2,1)S(1)}, u32[]{:S(2)}, u32[]{:S(2)}) collective-permute-start(bf16[256,128]{1,0:T(8,128)(2,1)S(1)} %get-tuple-element.62.refs_0_), channel_id=1, source_target_pairs={{0,34},{2,36},{4,38},{6,32},{32,2},{34,4},{36,6},{38,0},{1,35},{3,... | collective-permute-start | bytes 196616 | tf_op jit(solution)/shard_map/ppermute | solution.py:462
  15.0 22.0 %collective-permute-start.3 = (bf16[256,128]{1,0:T(8,128)(2,1)S(1)}, bf16[256,128]{1,0:T(8,128)(2,1)S(1)}, u32[]{:S(2)}, u32[]{:S(2)}) collective-permute-start(bf16[256,128]{1,0:T(8,128)(2,1)S(1)} %get-tuple-element.62.refs_0_), channel_id=1, source_target_pairs={{0,4},{2,6},{4,0},{6,2},{32,36},{34,38},{36,32},{38,34},{1,5},{3,7... | collective-permute-start | bytes 196616 | tf_op jit(solution)/shard_map/ppermute | solution.py:462
  16.5 20.6 %collective-permute-start.4 = (bf16[256,128]{1,0:T(8,128)(2,1)S(1)}, bf16[256,128]{1,0:T(8,128)(2,1)S(1)}, u32[]{:S(2)}, u32[]{:S(2)}) collective-permute-start(bf16[256,128]{1,0:T(8,128)(2,1)S(1)} %get-tuple-element.62.refs_0_), channel_id=1, source_target_pairs={{0,36},{2,38},{4,32},{6,34},{32,4},{34,6},{36,0},{38,2},{1,37},{3,... | collective-permute-start | bytes 196616 | tf_op jit(solution)/shard_map/ppermute | solution.py:462
  33.2 3.8 %collective-permute-start.5 = (bf16[256,128]{1,0:T(8,128)(2,1)S(1)}, bf16[256,128]{1,0:T(8,128)(2,1)S(1)}, u32[]{:S(2)}, u32[]{:S(2)}) collective-permute-start(bf16[256,128]{1,0:T(8,128)(2,1)S(1)} %get-tuple-element.62.refs_0_), channel_id=1, source_target_pairs={{0,6},{2,0},{4,2},{6,4},{32,38},{34,32},{36,34},{38,36},{1,7},{3,1... | collective-permute-start | bytes 196616 | tf_op jit(solution)/shard_map/ppermute | solution.py:462
  35.7 4.1 %collective-permute-start.6 = (bf16[256,128]{1,0:T(8,128)(2,1)S(1)}, bf16[256,128]{1,0:T(8,128)(2,1)S(1)}, u32[]{:S(2)}, u32[]{:S(2)}) collective-permute-start(bf16[256,128]{1,0:T(8,128)(2,1)S(1)} %get-tuple-element.62.refs_0_), channel_id=1, source_target_pairs={{0,38},{2,32},{4,34},{6,36},{32,6},{34,0},{36,2},{38,4},{1,39},{3,... | collective-permute-start | bytes 196616 | tf_op jit(solution)/shard_map/ppermute | solution.py:462
  39.8 5.9 %collective-permute-start.7 = (bf16[2048,384]{1,0:T(8,128)(2,1)S(1)}, bf16[2048,384]{1,0:T(8,128)(2,1)S(1)}, u32[]{:S(2)}, u32[]{:S(2)}) collective-permute-start(bf16[2048,384]{1,0:T(8,128)(2,1)S(1)} %bitcast.36), channel_id=1, source_target_pairs={{0,1},{1,0},{2,3},{3,2},{4,5},{5,4},{6,7},{7,6},{8,9},{9,8},{10,11... | collective-permute-start | bytes 4718600 | tf_op jit(solution)/shard_map/ppermute | solution.py:469
  47.6 17.5 %collective-permute-start.8 = (f32[256,256]{1,0:T(8,128)S(1)}, f32[256,256]{1,0:T(8,128)S(1)}, u32[]{:S(2)}, u32[]{:S(2)}) collective-permute-start(f32[256,256]{1,0:T(8,128)S(1)} %get-tuple-element.77), channel_id=1, source_target_pairs={{0,36},{2,38},{4,32},{6,34},{32,4},{34,6},{36,0},{38,2},{1,37},{3,... | collective-permute-start | bytes 786440 | tf_op jit(solution)/shard_map/ppermute | solution.py:462
  49.0 16.2 %collective-permute-start.9 = (f32[256,256]{1,0:T(8,128)S(1)}, f32[256,256]{1,0:T(8,128)S(1)}, u32[]{:S(2)}, u32[]{:S(2)}) collective-permute-start(f32[256,256]{1,0:T(8,128)S(1)} %get-tuple-element.78), channel_id=1, source_target_pairs={{0,4},{2,6},{4,0},{6,2},{32,36},{34,38},{36,32},{38,34},{1,5},{3,7... | collective-permute-start | bytes 786440 | tf_op jit(solution)/shard_map/ppermute | solution.py:462
  54.9 25.3 %copy-start = (bf16[256,256]{1,0:T(8,128)(2,1)S(1)}, bf16[256,256]{1,0:T(8,128)(2,1)}, u32[]{:S(2)}) copy-start(bf16[256,256]{1,0:T(8,128)(2,1)} %refs_8_.1) | copy-start | bytes 393220
  54.9 25.3 %copy-start.1 = (f32[256]{0:T(256)S(1)}, f32[256]{0:T(256)}, u32[]{:S(2)}) copy-start(f32[256]{0:T(256)} %param.8) | copy-start | bytes 3076
  58.0 12.6 %collective-permute-start.10 = (f32[256,256]{1,0:T(8,128)S(1)}, f32[256,256]{1,0:T(8,128)S(1)}, u32[]{:S(2)}, u32[]{:S(2)}) collective-permute-start(f32[256,256]{1,0:T(8,128)S(1)} %get-tuple-element.79), channel_id=1, source_target_pairs={{0,38},{2,32},{4,34},{6,36},{32,6},{34,0},{36,2},{38,4},{1,39},{3,... | collective-permute-start | bytes 786440 | tf_op jit(solution)/shard_map/ppermute | solution.py:462
  60.0 15.6 %collective-permute-start.11 = (f32[256,256]{1,0:T(8,128)S(1)}, f32[256,256]{1,0:T(8,128)S(1)}, u32[]{:S(2)}, u32[]{:S(2)}) collective-permute-start(f32[256,256]{1,0:T(8,128)S(1)} %get-tuple-element.80), channel_id=1, source_target_pairs={{0,6},{2,0},{4,2},{6,4},{32,38},{34,32},{36,34},{38,36},{1,7},{3,1... | collective-permute-start | bytes 786440 | tf_op jit(solution)/shard_map/ppermute | solution.py:462
  61.4 14.2 %collective-permute-start.12 = (f32[256,256]{1,0:T(8,128)S(1)}, f32[256,256]{1,0:T(8,128)S(1)}, u32[]{:S(2)}, u32[]{:S(2)}) collective-permute-start(f32[256,256]{1,0:T(8,128)S(1)} %get-tuple-element.81), channel_id=1, source_target_pairs={{0,34},{2,36},{4,38},{6,32},{32,2},{34,4},{36,6},{38,0},{1,35},{3,... | collective-permute-start | bytes 786440 | tf_op jit(solution)/shard_map/ppermute | solution.py:462
  65.1 12.0 %collective-permute-start.13 = (f32[256,256]{1,0:T(8,128)S(1)}, f32[256,256]{1,0:T(8,128)S(1)}, u32[]{:S(2)}, u32[]{:S(2)}) collective-permute-start(f32[256,256]{1,0:T(8,128)S(1)} %get-tuple-element.82), channel_id=1, source_target_pairs={{0,2},{2,4},{4,6},{6,0},{32,34},{34,36},{36,38},{38,32},{1,3},{3,5... | collective-permute-start | bytes 786440 | tf_op jit(solution)/shard_map/ppermute | solution.py:462
  65.2 15.0 %collective-permute-start.14 = (f32[256,256]{1,0:T(8,128)S(1)}, f32[256,256]{1,0:T(8,128)S(1)}, u32[]{:S(2)}, u32[]{:S(2)}) collective-permute-start(f32[256,256]{1,0:T(8,128)S(1)} %get-tuple-element.83), channel_id=1, source_target_pairs={{0,32},{2,34},{4,36},{6,38},{32,0},{34,2},{36,4},{38,6},{1,33},{3,... | collective-permute-start | bytes 786440 | tf_op jit(solution)/shard_map/ppermute | solution.py:462

commit v3 on v2

--- a/solution.py
+++ b/solution.py
@@ -16,6 +16,7 @@
 ROWS = ("row_1", "col_0")
 LOG2E = 1.4426950408889634
 MIB = 1024 * 1024
+WIDTH = 16
 F32 = jnp.float32
 BF16 = jnp.bfloat16
 HIGH = lax.Precision.HIGHEST
@@ -194,21 +195,22 @@
 
 def inverted(work_ref):
     size = work_ref.shape[0]
-    panels = size // 8
-    sub = lax.broadcasted_iota(jnp.int32, (8, 1), 0)
+    panels = size // WIDTH
+    per_window = 128 // WIDTH
+    sub = lax.broadcasted_iota(jnp.int32, (WIDTH, 1), 0)
     lanes = lax.broadcasted_iota(jnp.int32, (1, size), 1)
 
     def column(block, step, j):
-        index = jnp.full((8, 128), 0, jnp.int32) + ((step % 16) * 8 + j)
-        window = jnp.where(step < 16, block[:, 0:128], block[:, 128:256])
+        index = jnp.full((WIDTH, 128), 0, jnp.int32) + ((step % per_window) * WIDTH + j)
+        window = jnp.where(step < per_window, block[:, 0:128], block[:, 128:256])
         return jnp.take_along_axis(window, index, axis=1)
 
     def wide(value):
         return jnp.concatenate([value, value], axis=1)
 
     def eliminated(panel, step):
-        diag = [column(panel, step, j) for j in range(8)]
-        for j in range(0, 8, 2):
+        diag = [column(panel, step, j) for j in range(WIDTH)]
+        for j in range(0, WIDTH, 2):
             a, b = diag[j][j : j + 1, :], diag[j + 1][j : j + 1, :]
             c, d = diag[j][j + 1 : j + 2, :], diag[j + 1][j + 1 : j + 2, :]
             inverse = 1.0 / (a * d - b * c)
@@ -221,10 +223,10 @@
                 rest = block - first * new_top - second * new_bottom
                 return jnp.where(upper, new_top, jnp.where(lower, new_bottom, rest))
 
-            for k in range(j + 2, 8):
+            for k in range(j + 2, WIDTH):
                 diag[k] = swept(diag[k], diag[j], diag[j + 1])
-            panel = jnp.where(lanes == step * 8 + j, jnp.where(upper, 1.0, 0.0), panel)
-            panel = jnp.where(lanes == step * 8 + j + 1, jnp.where(lower, 1.0, 0.0), panel)
+            panel = jnp.where(lanes == step * WIDTH + j, jnp.where(upper, 1.0, 0.0), panel)
+            panel = jnp.where(lanes == step * WIDTH + j + 1, jnp.where(lower, 1.0, 0.0), panel)
             panel = swept(panel, wide(diag[j]), wide(diag[j + 1]), wide)
         return panel
 
@@ -237,11 +239,11 @@
     def panel_step(step, carry):
         panel, factors = carry
         following = jnp.minimum(step + 1, panels - 1)
-        here = pl.ds(pl.multiple_of(step * 8, 8), 8)
-        ahead = work_ref[pl.ds(pl.multiple_of(following * 8, 8), 8), :]
-        inside = (lanes >= step * 8) & (lanes < step * 8 + 8)
+        here = pl.ds(pl.multiple_of(step * WIDTH, WIDTH), WIDTH)
+        ahead = work_ref[pl.ds(pl.multiple_of(following * WIDTH, WIDTH), WIDTH), :]
+        inside = (lanes >= step * WIDTH) & (lanes < step * WIDTH + WIDTH)
         following_rows = jnp.where(inside, 0.0, ahead)
-        for j in range(8):
+        for j in range(WIDTH):
             following_rows = following_rows - wide(column(ahead, step, j)) * panel[j : j + 1, :]
         f1, f2, f3 = split(factors)
         p1, p2, p3 = split(panel)
@@ -253,10 +255,10 @@
         )
         work_ref[...] = jnp.where(inside, 0.0, work_ref[...]) - update
         work_ref[here, :] = panel
-        following_factors = jnp.where(lanes < following * 8, -following_rows, following_rows)
+        following_factors = jnp.where(lanes < following * WIDTH, -following_rows, following_rows)
         return eliminated(following_rows, following), following_factors
 
-    start = work_ref[0:8, :]
+    start = work_ref[0:WIDTH, :]
     lax.fori_loop(0, panels, panel_step, (eliminated(start, 0), start))
 
 
@@ -468,19 +470,26 @@
     message, chunks = lax.optimization_barrier((message, chunks))
     partner = lax.ppermute(message, "col_1", [(0, 1), (1, 0)])
     norm = call(norms_body, shape(8, message.shape[0]), message)
-    kerns, before, sums = [], [], []
-    for shift in ORDER:
-        kern, *sketches = kernel_block(chunks[shift, 0], chunks[shift, 1], message, norm)
-        kerns.append(kern)
-        before.append(sketches)
-    norm = call(norms_body, shape(8, message.shape[0]), partner)
+    kerns, before, sums = {}, {}, []
+
+    def near_block(number):
+        shift = ORDER[number]
+        kerns[number], *before[number] = kernel_block(
+            chunks[shift, 0], chunks[shift, 1], message, norm
+        )
+
+    for number in range(3):
+        near_block(number)
+    other_norm = call(norms_body, shape(8, message.shape[0]), partner)
     for number, shift in enumerate(ORDER):
-        kern, *sketches = kernel_block(
-            chunks[shift, 0], chunks[shift, 1], partner, norm, before[number]
+        if number == 3:
+            near_block(number)
+        kerns[number + 4], *sketches = kernel_block(
+            chunks[shift, 0], chunks[shift, 1], partner, other_norm, before[number]
         )
-        kerns.append(kern)
         for flip in (1, 0):
             sums.append(along_rows(sketches[flip], -shift, flip))
+    kerns = [kerns[i] for i in range(8)]
     sketch_out, sketch, packed = call(
         core_body,
         [shape(own, rank), shape(own, rank), shape(everyone, 512)],

time: 197 us -> 196 us (level)
  no operation moved by 1% of the time
where the time goes in v3:
time: 196 us
  blocking collectives  97.5 us (50%)
  Pallas kernels  32.8 us (17%)
  waiting for transfers between devices  32.5 us (17%)
  starting transfers between devices  30.5 us (16%)
    all_to_all x7, blocking collectives, exchanged(): return lax.all_to_all(pieces, axes, 0, 0, tiled=True)  97.5 us
    ppermute x14, waiting for transfers between devices, along_rows(): return lax.ppermute(value, ROWS, pairs) if shift or flip else value  31.7 us
    pallas_call x18, Pallas kernels, call(): pl.pallas_call(body, out_shape=outs, scratch_shapes=list(scratch), compil...  30.5 us
    ppermute x14, starting transfers between devices, along_rows(): return lax.ppermute(value, ROWS, pairs) if shift or flip else value  19.1 us
    all_to_all x1, starting transfers between devices, exchanged(): return lax.all_to_all(pieces, axes, 0, 0, tiled=True)  8.49 us
  transfers between devices with their start and end apart: 16, of which 7 were waited for; matrix products, arithmetic and copies ran while one was open for 0% of the time, Pallas kernels for 6%

profile of v3, /device:TPU:1, one launch (start us, length us, event | category | flops | bytes accessed | tf_op | source)
XLA Modules:
  0.0 196.0 jit_solution(13693982765078702992)
XLA Ops:
  0.6 2.3 %parts.1 = (bf16[256,128]{1,0:T(8,128)(2,1)S(1)}, bf16[8,256,384]{2,1,0:T(8,128)(2,1)}) custom-call(f32[64,256]{1,0:T(8,128)} %bitcast.60, f32[1,64]{1,0:T(1,128)} %bitcast.61, bf16[256,256]{1,0:T(8,128)(2,1)} %refs_8_.1), custom_call_target="tpu_custom_call" | custom-call | tf_op jit(solution)/shard_map/parts/pallas_call | solution.py:88
  2.9 8.5 %all-to-all-start = ((bf16[8,256,384]{2,1,0:T(8,128)(2,1)}), bf16[8,256,384]{2,1,0:T(8,128)(2,1)S(1)}, u32[]{:S(2)}, u32[]{:S(2)}) async-start(bf16[8,256,384]{2,1,0:T(8,128)(2,1)} %get-tuple-element.50), calls=%async_computation | async-start | bytes 3145728 | tf_op jit(solution)/shard_map/all_to_all | solution.py:43
  13.0 2.0 %collective-permute-start.2 = (bf16[256,128]{1,0:T(8,128)(2,1)S(1)}, bf16[256,128]{1,0:T(8,128)(2,1)S(1)}, u32[]{:S(2)}, u32[]{:S(2)}) collective-permute-start(bf16[256,128]{1,0:T(8,128)(2,1)S(1)} %get-tuple-element.62.refs_0_), channel_id=1, source_target_pairs={{0,34},{2,36},{4,38},{6,32},{32,2},{34,4},{36,6},{38,0},{1,35},{3,... | collective-permute-start | bytes 196616 | tf_op jit(solution)/shard_map/ppermute | solution.py:464
  15.0 1.4 collective-permute-start.3
  16.5 1.6 collective-permute-start.4
  18.1 15.1 %collective-permute-done.refs_1_ = bf16[256,128]{1,0:T(8,128)(2,1)S(1)} collective-permute-done((bf16[256,128]{1,0:T(8,128)(2,1)S(1)}, bf16[256,128]{1,0:T(8,128)(2,1)S(1)}, u32[]{:S(2)}, u32[]{:S(2)}) %collective-permute-start) | collective-permute-done | bytes 65568 | tf_op jit(solution)/shard_map/ppermute | solution.py:464
  33.2 2.5 %collective-permute-start.5 = (bf16[256,128]{1,0:T(8,128)(2,1)S(1)}, bf16[256,128]{1,0:T(8,128)(2,1)S(1)}, u32[]{:S(2)}, u32[]{:S(2)}) collective-permute-start(bf16[256,128]{1,0:T(8,128)(2,1)S(1)} %get-tuple-element.62.refs_0_), channel_id=1, source_target_pairs={{0,6},{2,0},{4,2},{6,4},{32,38},{34,32},{36,34},{38,36},{1,7},{3,1... | collective-permute-start | bytes 196616 | tf_op jit(solution)/shard_map/ppermute | solution.py:464
  37.1 2.8 %collective-permute-done.6.refs_1_ = bf16[256,128]{1,0:T(8,128)(2,1)S(1)} collective-permute-done((bf16[256,128]{1,0:T(8,128)(2,1)S(1)}, bf16[256,128]{1,0:T(8,128)(2,1)S(1)}, u32[]{:S(2)}, u32[]{:S(2)}) %collective-permute-start.6) | collective-permute-done | bytes 65568 | tf_op jit(solution)/shard_map/ppermute | solution.py:464
  39.8 2.9 %collective-permute-start.7 = (bf16[2048,384]{1,0:T(8,128)(2,1)S(1)}, bf16[2048,384]{1,0:T(8,128)(2,1)S(1)}, u32[]{:S(2)}, u32[]{:S(2)}) collective-permute-start(bf16[2048,384]{1,0:T(8,128)(2,1)S(1)} %bitcast.36), channel_id=1, source_target_pairs={{0,1},{1,0},{2,3},{3,2},{4,5},{5,4},{6,7},{7,6},{8,9},{9,8},{10,11... | collective-permute-start | bytes 4718600 | tf_op jit(solution)/shard_map/ppermute | solution.py:471
  43.2 1.7 shard_map.77
  46.2 1.4 shard_map.82
  49.0 2.5 %collective-permute-start.9 = (f32[256,256]{1,0:T(8,128)S(1)}, f32[256,256]{1,0:T(8,128)S(1)}, u32[]{:S(2)}, u32[]{:S(2)}) collective-permute-start(f32[256,256]{1,0:T(8,128)S(1)} %get-tuple-element.78), channel_id=1, source_target_pairs={{0,4},{2,6},{4,0},{6,2},{32,36},{34,38},{36,32},{38,34},{1,5},{3,7... | collective-permute-start | bytes 786440 | tf_op jit(solution)/shard_map/ppermute | solution.py:464
  51.5 1.7 shard_map.78
  53.2 1.7 shard_map.79
  54.9 1.7 shard_map.80
  56.6 1.4 shard_map.83
  58.0 1.9 collective-permute-start.10
  61.4 2.3 %collective-permute-start.12 = (f32[256,256]{1,0:T(8,128)S(1)}, f32[256,256]{1,0:T(8,128)S(1)}, u32[]{:S(2)}, u32[]{:S(2)}) collective-permute-start(f32[256,256]{1,0:T(8,128)S(1)} %get-tuple-element.81), channel_id=1, source_target_pairs={{0,34},{2,36},{4,38},{6,32},{32,2},{34,4},{36,6},{38,0},{1,35},{3,... | collective-permute-start | bytes 786440 | tf_op jit(solution)/shard_map/ppermute | solution.py:464
  66.3 4.2 %collective-permute-done.10.refs_2_ = f32[256,256]{1,0:T(8,128)S(1)} collective-permute-done((f32[256,256]{1,0:T(8,128)S(1)}, f32[256,256]{1,0:T(8,128)S(1)}, u32[]{:S(2)}, u32[]{:S(2)}) %collective-permute-start.10) | collective-permute-done | bytes 262176 | tf_op jit(solution)/shard_map/ppermute | solution.py:464
  70.6 5.0 %collective-permute-done.11.refs_3_ = f32[256,256]{1,0:T(8,128)S(1)} collective-permute-done((f32[256,256]{1,0:T(8,128)S(1)}, f32[256,256]{1,0:T(8,128)S(1)}, u32[]{:S(2)}, u32[]{:S(2)}) %collective-permute-start.11) | collective-permute-done | bytes 262176 | tf_op jit(solution)/shard_map/ppermute | solution.py:464
  75.6 1.6 collective-permute-done.13.refs_5_
  77.1 3.1 %collective-permute-done.14.refs_6_ = f32[256,256]{1,0:T(8,128)S(1)} collective-permute-done((f32[256,256]{1,0:T(8,128)S(1)}, f32[256,256]{1,0:T(8,128)S(1)}, u32[]{:S(2)}, u32[]{:S(2)}) %collective-permute-start.14) | collective-permute-done | bytes 262176 | tf_op jit(solution)/shard_map/ppermute | solution.py:464
  81.4 19.6 %all_to_all.76 = f32[128,1,512]{2,1,0:T(1,128)S(1)} all-to-all(f32[128,1,512]{2,1,0:T(1,128)S(1)} %copy.8), channel_id=1, replica_groups=mesh['row_0'=2,'row_1'=2,'row_2'=4,'col_0'=4,'col_1'=2] {'col_0','col_1'..., dimensions={0} | all-to-all | bytes 524288 | tf_op jit(solution)/shard_map/all_to_all | solution.py:43
  101.3 15.2 %all_to_all.77 = f32[128,1,512]{2,1,0:T(1,128)S(1)} all-to-all(f32[128,1,512]{2,1,0:T(1,128)S(1)} %copy.9), channel_id=1, replica_groups=mesh['row_0'=2,'row_1'=2,'row_2'=4,'col_0'=4,'col_1'=2] {'col_0','col_1'..., dimensions={0} | all-to-all | bytes 524288 | tf_op jit(solution)/shard_map/all_to_all | solution.py:43
  116.5 9.4 %shard_map.88 = (f32[256,256]{1,0:T(8,128)S(1)}, f32[8,256]{1,0:T(8,128)S(1)}, f32[16,256]{1,0:T(8,128)S(1)}) custom-call(f32[128,512]{1,0:T(8,128)S(1)} %bitcast.44, f32[256,256]{1,0:T(8,128)S(1)} %get-tuple-element.86.sketch_ref, f32[1,256]{1,0:T(1,128)S(1)} %bitcast.55, f32[1,1]{1,0:T(1,128)} %bitcast.32.ridge_ref), custom_call_target="tpu_custom_call" | custom-call | tf_op jit(solution)/shard_map/pallas_call | solution.py:30
  126.0 10.6 %all_to_all.78 = f32[16,1,256]{2,1,0:T(1,128)S(1)} all-to-all(f32[16,1,256]{2,1,0:T(1,128)S(1)} %copy.10), channel_id=1, replica_groups=mesh['row_0'=2,'row_1'=2,'row_2'=4,'col_0'=4,'col_1'=2] {'col_1','row_0'..., dimensions={0} | all-to-all | bytes 32768 | tf_op jit(solution)/shard_map/all_to_all | solution.py:43
  136.6 2.4 %shard_map.89 = f32[8,8,256]{2,1,0:T(8,128)S(1)} custom-call(f32[512,2048]{1,0:T(8,128)S(1)} %get-tuple-element.55.refs_0_, f32[512,2048]{1,0:T(8,128)S(1)} %get-tuple-element.58.refs_1_, f32[512,2048]{1,0:T(8,128)S(1)} %get-tuple-element.61.refs_2_, f32[512,2048]{1,0:T(8,128)S(1)} %get-tuple-element.64.refs_3_, f32[512,2048]{1,0:T(8,128)S(1)} %get-tuple-element.67.refs_4_, ...), custom_call_target="tpu_custom_call" | custom-call | tf_op jit(solution)/shard_map/pallas_call | solution.py:30
  139.0 7.7 %all_to_all.79.parts_ref = f32[8,8,256]{2,1,0:T(8,128)S(1)} all-to-all(f32[8,8,256]{2,1,0:T(8,128)S(1)} %shard_map.89), channel_id=1, replica_groups=mesh['row_0'=2,'row_1'=2,'row_2'=4,'col_0'=4,'col_1'=2] {'row_1','col_0'}, dimensions={0} | all-to-all | bytes 131072 | tf_op jit(solution)/shard_map/all_to_all | solution.py:43
  147.2 15.6 %all_to_all.80 = f32[128,1,384]{2,1,0:T(1,128)S(1)} all-to-all(f32[128,1,384]{2,1,0:T(1,128)S(1)} %copy.11), channel_id=1, replica_groups=mesh['row_0'=2,'row_1'=2,'row_2'=4,'col_0'=4,'col_1'=2] {'col_0','col_1'..., dimensions={0} | all-to-all | bytes 393216 | tf_op jit(solution)/shard_map/all_to_all | solution.py:43
  163.8 14.2 %all_to_all.81 = f32[128,1,256]{2,1,0:T(1,128)S(1)} all-to-all(f32[128,1,256]{2,1,0:T(1,128)S(1)} %copy.12), channel_id=1, replica_groups=mesh['row_0'=2,'row_1'=2,'row_2'=4,'col_0'=4,'col_1'=2] {'col_0','col_1'..., dimensions={0} | all-to-all | bytes 262144 | tf_op jit(solution)/shard_map/all_to_all | solution.py:43
  178.0 2.6 %shard_map.92 = f32[128,384]{1,0:T(8,128)S(1)} custom-call(f32[512,2048]{1,0:T(8,128)S(1)} %get-tuple-element.55.refs_0_, f32[512,2048]{1,0:T(8,128)S(1)} %get-tuple-element.58.refs_1_, f32[512,2048]{1,0:T(8,128)S(1)} %get-tuple-element.61.refs_2_, f32[512,2048]{1,0:T(8,128)S(1)} %get-tuple-element.64.refs_3_, f32[512,2048]{1,0:T(8,128)S(1)} %get-tuple-element.67.refs_4_, ...), custom_call_target="tpu_custom_call" | custom-call | tf_op jit(solution)/shard_map/pallas_call | solution.py:30
  180.8 14.6 %all_to_all.82 = f32[128,1,384]{2,1,0:T(1,128)S(1)} all-to-all(f32[128,1,384]{2,1,0:T(1,128)S(1)} %copy.13), channel_id=1, replica_groups=mesh['row_0'=2,'row_1'=2,'row_2'=4,'col_0'=4,'col_1'=2] {'col_0','col_1'..., dimensions={0} | all-to-all | bytes 393216 | tf_op jit(solution)/shard_map/all_to_all | solution.py:43
  (42 shorter events, 13.4 us)
Async XLA Ops:
  2.9 36.9 %all-to-all-start = ((bf16[8,256,384]{2,1,0:T(8,128)(2,1)}), bf16[8,256,384]{2,1,0:T(8,128)(2,1)S(1)}, u32[]{:S(2)}, u32[]{:S(2)}) async-start(bf16[8,256,384]{2,1,0:T(8,128)(2,1)} %get-tuple-element.50), calls=%async_computation | async-start | bytes 3145728 | tf_op jit(solution)/shard_map/all_to_all | solution.py:43
  11.4 21.8 %collective-permute-start = (bf16[256,128]{1,0:T(8,128)(2,1)S(1)}, bf16[256,128]{1,0:T(8,128)(2,1)S(1)}, u32[]{:S(2)}, u32[]{:S(2)}) collective-permute-start(bf16[256,128]{1,0:T(8,128)(2,1)S(1)} %get-tuple-element.62.refs_0_), channel_id=1, source_target_pairs={{0,32},{2,34},{4,36},{6,38},{32,0},{34,2},{36,4},{38,6},{1,33},{3,... | collective-permute-start | bytes 196616 | tf_op jit(solution)/shard_map/ppermute | solution.py:464
  11.8 23.9 %collective-permute-start.1 = (bf16[256,128]{1,0:T(8,128)(2,1)S(1)}, bf16[256,128]{1,0:T(8,128)(2,1)S(1)}, u32[]{:S(2)}, u32[]{:S(2)}) collective-permute-start(bf16[256,128]{1,0:T(8,128)(2,1)S(1)} %get-tuple-element.62.refs_0_), channel_id=1, source_target_pairs={{0,2},{2,4},{4,6},{6,0},{32,34},{34,36},{36,38},{38,32},{1,3},{3,5... | collective-permute-start | bytes 196616 | tf_op jit(solution)/shard_map/ppermute | solution.py:464
  13.0 24.0 %collective-permute-start.2 = (bf16[256,128]{1,0:T(8,128)(2,1)S(1)}, bf16[256,128]{1,0:T(8,128)(2,1)S(1)}, u32[]{:S(2)}, u32[]{:S(2)}) collective-permute-start(bf16[256,128]{1,0:T(8,128)(2,1)S(1)} %get-tuple-element.62.refs_0_), channel_id=1, source_target_pairs={{0,34},{2,36},{4,38},{6,32},{32,2},{34,4},{36,6},{38,0},{1,35},{3,... | collective-permute-start | bytes 196616 | tf_op jit(solution)/shard_map/ppermute | solution.py:464
  15.0 22.0 %collective-permute-start.3 = (bf16[256,128]{1,0:T(8,128)(2,1)S(1)}, bf16[256,128]{1,0:T(8,128)(2,1)S(1)}, u32[]{:S(2)}, u32[]{:S(2)}) collective-permute-start(bf16[256,128]{1,0:T(8,128)(2,1)S(1)} %get-tuple-element.62.refs_0_), channel_id=1, source_target_pairs={{0,4},{2,6},{4,0},{6,2},{32,36},{34,38},{36,32},{38,34},{1,5},{3,7... | collective-permute-start | bytes 196616 | tf_op jit(solution)/shard_map/ppermute | solution.py:464
  16.5 20.6 %collective-permute-start.4 = (bf16[256,128]{1,0:T(8,128)(2,1)S(1)}, bf16[256,128]{1,0:T(8,128)(2,1)S(1)}, u32[]{:S(2)}, u32[]{:S(2)}) collective-permute-start(bf16[256,128]{1,0:T(8,128)(2,1)S(1)} %get-tuple-element.62.refs_0_), channel_id=1, source_target_pairs={{0,36},{2,38},{4,32},{6,34},{32,4},{34,6},{36,0},{38,2},{1,37},{3,... | collective-permute-start | bytes 196616 | tf_op jit(solution)/shard_map/ppermute | solution.py:464
  33.2 3.8 %collective-permute-start.5 = (bf16[256,128]{1,0:T(8,128)(2,1)S(1)}, bf16[256,128]{1,0:T(8,128)(2,1)S(1)}, u32[]{:S(2)}, u32[]{:S(2)}) collective-permute-start(bf16[256,128]{1,0:T(8,128)(2,1)S(1)} %get-tuple-element.62.refs_0_), channel_id=1, source_target_pairs={{0,6},{2,0},{4,2},{6,4},{32,38},{34,32},{36,34},{38,36},{1,7},{3,1... | collective-permute-start | bytes 196616 | tf_op jit(solution)/shard_map/ppermute | solution.py:464
  35.7 4.1 %collective-permute-start.6 = (bf16[256,128]{1,0:T(8,128)(2,1)S(1)}, bf16[256,128]{1,0:T(8,128)(2,1)S(1)}, u32[]{:S(2)}, u32[]{:S(2)}) collective-permute-start(bf16[256,128]{1,0:T(8,128)(2,1)S(1)} %get-tuple-element.62.refs_0_), channel_id=1, source_target_pairs={{0,38},{2,32},{4,34},{6,36},{32,6},{34,0},{36,2},{38,4},{1,39},{3,... | collective-permute-start | bytes 196616 | tf_op jit(solution)/shard_map/ppermute | solution.py:464
  39.8 5.9 %collective-permute-start.7 = (bf16[2048,384]{1,0:T(8,128)(2,1)S(1)}, bf16[2048,384]{1,0:T(8,128)(2,1)S(1)}, u32[]{:S(2)}, u32[]{:S(2)}) collective-permute-start(bf16[2048,384]{1,0:T(8,128)(2,1)S(1)} %bitcast.36), channel_id=1, source_target_pairs={{0,1},{1,0},{2,3},{3,2},{4,5},{5,4},{6,7},{7,6},{8,9},{9,8},{10,11... | collective-permute-start | bytes 4718600 | tf_op jit(solution)/shard_map/ppermute | solution.py:471
  47.6 17.5 %collective-permute-start.8 = (f32[256,256]{1,0:T(8,128)S(1)}, f32[256,256]{1,0:T(8,128)S(1)}, u32[]{:S(2)}, u32[]{:S(2)}) collective-permute-start(f32[256,256]{1,0:T(8,128)S(1)} %get-tuple-element.77), channel_id=1, source_target_pairs={{0,36},{2,38},{4,32},{6,34},{32,4},{34,6},{36,0},{38,2},{1,37},{3,... | collective-permute-start | bytes 786440 | tf_op jit(solution)/shard_map/ppermute | solution.py:464
  49.0 16.2 %collective-permute-start.9 = (f32[256,256]{1,0:T(8,128)S(1)}, f32[256,256]{1,0:T(8,128)S(1)}, u32[]{:S(2)}, u32[]{:S(2)}) collective-permute-start(f32[256,256]{1,0:T(8,128)S(1)} %get-tuple-element.78), channel_id=1, source_target_pairs={{0,4},{2,6},{4,0},{6,2},{32,36},{34,38},{36,32},{38,34},{1,5},{3,7... | collective-permute-start | bytes 786440 | tf_op jit(solution)/shard_map/ppermute | solution.py:464
  54.9 25.3 %copy-start = (bf16[256,256]{1,0:T(8,128)(2,1)S(1)}, bf16[256,256]{1,0:T(8,128)(2,1)}, u32[]{:S(2)}) copy-start(bf16[256,256]{1,0:T(8,128)(2,1)} %refs_8_.1) | copy-start | bytes 393220
  54.9 25.3 %copy-start.1 = (f32[256]{0:T(256)S(1)}, f32[256]{0:T(256)}, u32[]{:S(2)}) copy-start(f32[256]{0:T(256)} %param.8) | copy-start | bytes 3076
  58.0 12.6 %collective-permute-start.10 = (f32[256,256]{1,0:T(8,128)S(1)}, f32[256,256]{1,0:T(8,128)S(1)}, u32[]{:S(2)}, u32[]{:S(2)}) collective-permute-start(f32[256,256]{1,0:T(8,128)S(1)} %get-tuple-element.79), channel_id=1, source_target_pairs={{0,38},{2,32},{4,34},{6,36},{32,6},{34,0},{36,2},{38,4},{1,39},{3,... | collective-permute-start | bytes 786440 | tf_op jit(solution)/shard_map/ppermute | solution.py:464
  60.0 15.6 %collective-permute-start.11 = (f32[256,256]{1,0:T(8,128)S(1)}, f32[256,256]{1,0:T(8,128)S(1)}, u32[]{:S(2)}, u32[]{:S(2)}) collective-permute-start(f32[256,256]{1,0:T(8,128)S(1)} %get-tuple-element.80), channel_id=1, source_target_pairs={{0,6},{2,0},{4,2},{6,4},{32,38},{34,32},{36,34},{38,36},{1,7},{3,1... | collective-permute-start | bytes 786440 | tf_op jit(solution)/shard_map/ppermute | solution.py:464
  61.4 14.2 %collective-permute-start.12 = (f32[256,256]{1,0:T(8,128)S(1)}, f32[256,256]{1,0:T(8,128)S(1)}, u32[]{:S(2)}, u32[]{:S(2)}) collective-permute-start(f32[256,256]{1,0:T(8,128)S(1)} %get-tuple-element.81), channel_id=1, source_target_pairs={{0,34},{2,36},{4,38},{6,32},{32,2},{34,4},{36,6},{38,0},{1,35},{3,... | collective-permute-start | bytes 786440 | tf_op jit(solution)/shard_map/ppermute | solution.py:464
  65.1 12.0 %collective-permute-start.13 = (f32[256,256]{1,0:T(8,128)S(1)}, f32[256,256]{1,0:T(8,128)S(1)}, u32[]{:S(2)}, u32[]{:S(2)}) collective-permute-start(f32[256,256]{1,0:T(8,128)S(1)} %get-tuple-element.82), channel_id=1, source_target_pairs={{0,2},{2,4},{4,6},{6,0},{32,34},{34,36},{36,38},{38,32},{1,3},{3,5... | collective-permute-start | bytes 786440 | tf_op jit(solution)/shard_map/ppermute | solution.py:464
  65.2 15.0 %collective-permute-start.14 = (f32[256,256]{1,0:T(8,128)S(1)}, f32[256,256]{1,0:T(8,128)S(1)}, u32[]{:S(2)}, u32[]{:S(2)}) collective-permute-start(f32[256,256]{1,0:T(8,128)S(1)} %get-tuple-element.83), channel_id=1, source_target_pairs={{0,32},{2,34},{4,36},{6,38},{32,0},{34,2},{36,4},{38,6},{1,33},{3,... | collective-permute-start | bytes 786440 | tf_op jit(solution)/shard_map/ppermute | solution.py:464

commit v4 on v3

--- a/solution.py
+++ b/solution.py
@@ -12,7 +12,6 @@
 AXES = ("row_0", "row_1", "row_2", "col_0", "col_1")
 ALL = ("col_0", "col_1", "row_0", "row_1", "row_2")
 NEAR_COLUMNS = ("row_0", "row_2")
-COLUMNS = ("col_1", "row_0", "row_2")
 ROWS = ("row_1", "col_0")
 LOG2E = 1.4426950408889634
 MIB = 1024 * 1024
@@ -337,10 +336,10 @@
 
 
 def product_body(*refs):
-    *kern_refs, vector_ref, out_ref = refs
+    *kern_refs, vector_ref, partner_ref, out_ref = refs
     half_y = lax.axis_index("row_1")
     chips = len(ORDER)
-    vector = own_first(vector_ref[0:8, :], vector_ref[8:16, :])
+    vector = jnp.concatenate([vector_ref[...], partner_ref[...]], axis=0)
     for shift, half, pieces in products(kern_refs, vector):
         span = slice(half * 128, half * 128 + 128)
         out_ref[half_y * chips + owner(shift), :, span] = eight(pieces[0])
@@ -377,7 +376,8 @@
 
 
 def kernel_times(kerns, vector):
-    return call(product_body, shape(8, 8, 256), *kerns, vector, limit=KLIMIT2)
+    partner = lax.ppermute(vector, "col_1", [(0, 1), (1, 0)])
+    return call(product_body, shape(8, 8, 256), *kerns, vector, partner, limit=KLIMIT2)
 
 
 def image_body(parts_ref, state_ref, sketch_ref, targets_ref, ridge_ref, image_ref, send_ref):
@@ -449,7 +449,7 @@
 
 def local(points, feature_scale, test_matrix, targets, ridge):
     everyone = lax.axis_size(ALL)
-    column_devices, near_devices = lax.axis_size(COLUMNS), lax.axis_size(NEAR_COLUMNS)
+    near_devices = lax.axis_size(NEAR_COLUMNS)
     own, rank = test_matrix.shape
     ridge = ridge.reshape(1, 1)
     targets = targets.reshape(1, own)
@@ -503,13 +503,13 @@
     packed = exchanged(packed, ALL)
     inverse, state, send = call(
         first_body,
-        [shape(rank, rank), shape(8, own), shape(column_devices, own)],
+        [shape(rank, rank), shape(8, own), shape(near_devices, own)],
         packed,
         sketch,
         targets,
         ridge,
     )
-    product = kernel_times(kerns, exchanged(send, COLUMNS))
+    product = kernel_times(kerns, exchanged(send, NEAR_COLUMNS))
     image, send = call(
         image_body,
         [shape(8, own), shape(everyone, 384)],

time: 196 us -> 198 us (1.010)
  starting transfers between devices: 30.5 us -> 32.5 us
  transfers between devices with their start and end apart: 16 -> 17, of which waited for: 7 -> 8; matrix products, arithmetic and copies ran while one was open for 0% -> 0% of each run, Pallas kernels for 6% -> 6%
where the time goes in v4:
time: 198 us
  blocking collectives  95.8 us (48%)
  waiting for transfers between devices  33.3 us (17%)
  Pallas kernels  33.2 us (17%)
  starting transfers between devices  32.5 us (16%)
    all_to_all x7, blocking collectives, exchanged(): return lax.all_to_all(pieces, axes, 0, 0, tiled=True)  95.8 us
    ppermute x14, waiting for transfers between devices, along_rows(): return lax.ppermute(value, ROWS, pairs) if shift or flip else value  31.7 us
    pallas_call x18, Pallas kernels, call(): pl.pallas_call(body, out_shape=outs, scratch_shapes=list(scratch), compil...  30.9 us
    ppermute x14, starting transfers between devices, along_rows(): return lax.ppermute(value, ROWS, pairs) if shift or flip else value  19.1 us
    all_to_all x1, starting transfers between devices, exchanged(): return lax.all_to_all(pieces, axes, 0, 0, tiled=True)  8.49 us
  transfers between devices with their start and end apart: 17, of which 8 were waited for; matrix products, arithmetic and copies ran while one was open for 0% of the time, Pallas kernels for 6%

profile of v4, /device:TPU:1, one launch (start us, length us, event | category | flops | bytes accessed | tf_op | source)
XLA Modules:
  0.0 197.5 jit_solution(15333398769178718976)
XLA Ops:
  0.6 2.3 %parts.1 = (bf16[256,128]{1,0:T(8,128)(2,1)S(1)}, bf16[8,256,384]{2,1,0:T(8,128)(2,1)}) custom-call(f32[64,256]{1,0:T(8,128)} %bitcast.61, f32[1,64]{1,0:T(1,128)} %bitcast.62, bf16[256,256]{1,0:T(8,128)(2,1)} %refs_8_.1), custom_call_target="tpu_custom_call" | custom-call | tf_op jit(solution)/shard_map/parts/pallas_call | solution.py:87
  2.9 8.5 %all-to-all-start = ((bf16[8,256,384]{2,1,0:T(8,128)(2,1)}), bf16[8,256,384]{2,1,0:T(8,128)(2,1)S(1)}, u32[]{:S(2)}, u32[]{:S(2)}) async-start(bf16[8,256,384]{2,1,0:T(8,128)(2,1)} %get-tuple-element.50), calls=%async_computation | async-start | bytes 3145728 | tf_op jit(solution)/shard_map/all_to_all | solution.py:42
  13.0 2.0 %collective-permute-start.2 = (bf16[256,128]{1,0:T(8,128)(2,1)S(1)}, bf16[256,128]{1,0:T(8,128)(2,1)S(1)}, u32[]{:S(2)}, u32[]{:S(2)}) collective-permute-start(bf16[256,128]{1,0:T(8,128)(2,1)S(1)} %get-tuple-element.62.refs_0_), channel_id=1, source_target_pairs={{0,34},{2,36},{4,38},{6,32},{32,2},{34,4},{36,6},{38,0},{1,35},{3,... | collective-permute-start | bytes 196616 | tf_op jit(solution)/shard_map/ppermute | solution.py:464
  15.0 1.4 collective-permute-start.3
  16.5 1.6 collective-permute-start.4
  18.1 15.1 %collective-permute-done.refs_1_ = bf16[256,128]{1,0:T(8,128)(2,1)S(1)} collective-permute-done((bf16[256,128]{1,0:T(8,128)(2,1)S(1)}, bf16[256,128]{1,0:T(8,128)(2,1)S(1)}, u32[]{:S(2)}, u32[]{:S(2)}) %collective-permute-start) | collective-permute-done | bytes 65568 | tf_op jit(solution)/shard_map/ppermute | solution.py:464
  33.2 2.5 %collective-permute-start.5 = (bf16[256,128]{1,0:T(8,128)(2,1)S(1)}, bf16[256,128]{1,0:T(8,128)(2,1)S(1)}, u32[]{:S(2)}, u32[]{:S(2)}) collective-permute-start(bf16[256,128]{1,0:T(8,128)(2,1)S(1)} %get-tuple-element.62.refs_0_), channel_id=1, source_target_pairs={{0,6},{2,0},{4,2},{6,4},{32,38},{34,32},{36,34},{38,36},{1,7},{3,1... | collective-permute-start | bytes 196616 | tf_op jit(solution)/shard_map/ppermute | solution.py:464
  37.1 2.8 %collective-permute-done.6.refs_1_ = bf16[256,128]{1,0:T(8,128)(2,1)S(1)} collective-permute-done((bf16[256,128]{1,0:T(8,128)(2,1)S(1)}, bf16[256,128]{1,0:T(8,128)(2,1)S(1)}, u32[]{:S(2)}, u32[]{:S(2)}) %collective-permute-start.6) | collective-permute-done | bytes 65568 | tf_op jit(solution)/shard_map/ppermute | solution.py:464
  39.8 2.9 %collective-permute-start.7 = (bf16[2048,384]{1,0:T(8,128)(2,1)S(1)}, bf16[2048,384]{1,0:T(8,128)(2,1)S(1)}, u32[]{:S(2)}, u32[]{:S(2)}) collective-permute-start(bf16[2048,384]{1,0:T(8,128)(2,1)S(1)} %bitcast.36), channel_id=1, source_target_pairs={{0,1},{1,0},{2,3},{3,2},{4,5},{5,4},{6,7},{7,6},{8,9},{9,8},{10,11... | collective-permute-start | bytes 4718600 | tf_op jit(solution)/shard_map/ppermute | solution.py:471
  43.2 1.7 shard_map.77
  46.2 1.4 shard_map.82
  49.0 2.4 %collective-permute-start.9 = (f32[256,256]{1,0:T(8,128)S(1)}, f32[256,256]{1,0:T(8,128)S(1)}, u32[]{:S(2)}, u32[]{:S(2)}) collective-permute-start(f32[256,256]{1,0:T(8,128)S(1)} %get-tuple-element.78), channel_id=1, source_target_pairs={{0,4},{2,6},{4,0},{6,2},{32,36},{34,38},{36,32},{38,34},{1,5},{3,7... | collective-permute-start | bytes 786440 | tf_op jit(solution)/shard_map/ppermute | solution.py:464
  51.5 1.7 shard_map.78
  53.2 1.7 shard_map.79
  54.9 1.7 shard_map.80
  58.0 1.9 collective-permute-start.10
  61.4 2.3 %collective-permute-start.12 = (f32[256,256]{1,0:T(8,128)S(1)}, f32[256,256]{1,0:T(8,128)S(1)}, u32[]{:S(2)}, u32[]{:S(2)}) collective-permute-start(f32[256,256]{1,0:T(8,128)S(1)} %get-tuple-element.81), channel_id=1, source_target_pairs={{0,34},{2,36},{4,38},{6,32},{32,2},{34,4},{36,6},{38,0},{1,35},{3,... | collective-permute-start | bytes 786440 | tf_op jit(solution)/shard_map/ppermute | solution.py:464
  66.3 4.3 %collective-permute-done.10.refs_2_ = f32[256,256]{1,0:T(8,128)S(1)} collective-permute-done((f32[256,256]{1,0:T(8,128)S(1)}, f32[256,256]{1,0:T(8,128)S(1)}, u32[]{:S(2)}, u32[]{:S(2)}) %collective-permute-start.10) | collective-permute-done | bytes 262176 | tf_op jit(solution)/shard_map/ppermute | solution.py:464
  70.6 5.0 %collective-permute-done.11.refs_3_ = f32[256,256]{1,0:T(8,128)S(1)} collective-permute-done((f32[256,256]{1,0:T(8,128)S(1)}, f32[256,256]{1,0:T(8,128)S(1)}, u32[]{:S(2)}, u32[]{:S(2)}) %collective-permute-start.11) | collective-permute-done | bytes 262176 | tf_op jit(solution)/shard_map/ppermute | solution.py:464
  75.6 1.5 collective-permute-done.13.refs_5_
  77.2 3.0 %collective-permute-done.14.refs_6_ = f32[256,256]{1,0:T(8,128)S(1)} collective-permute-done((f32[256,256]{1,0:T(8,128)S(1)}, f32[256,256]{1,0:T(8,128)S(1)}, u32[]{:S(2)}, u32[]{:S(2)}) %collective-permute-start.14) | collective-permute-done | bytes 262176 | tf_op jit(solution)/shard_map/ppermute | solution.py:464
  81.4 19.6 %all_to_all.76 = f32[128,1,512]{2,1,0:T(1,128)S(1)} all-to-all(f32[128,1,512]{2,1,0:T(1,128)S(1)} %copy.8), channel_id=1, replica_groups=mesh['row_0'=2,'row_1'=2,'row_2'=4,'col_0'=4,'col_1'=2] {'col_0','col_1'..., dimensions={0} | all-to-all | bytes 524288 | tf_op jit(solution)/shard_map/all_to_all | solution.py:42
  101.3 15.2 %all_to_all.77 = f32[128,1,512]{2,1,0:T(1,128)S(1)} all-to-all(f32[128,1,512]{2,1,0:T(1,128)S(1)} %copy.9), channel_id=1, replica_groups=mesh['row_0'=2,'row_1'=2,'row_2'=4,'col_0'=4,'col_1'=2] {'col_0','col_1'..., dimensions={0} | all-to-all | bytes 524288 | tf_op jit(solution)/shard_map/all_to_all | solution.py:42
  116.6 9.4 %shard_map.88 = (f32[256,256]{1,0:T(8,128)S(1)}, f32[8,256]{1,0:T(8,128)S(1)}, f32[8,256]{1,0:T(8,128)S(1)}) custom-call(f32[128,512]{1,0:T(8,128)S(1)} %bitcast.44, f32[256,256]{1,0:T(8,128)S(1)} %get-tuple-element.86.sketch_ref, f32[1,256]{1,0:T(1,128)S(1)} %bitcast.56, f32[1,1]{1,0:T(1,128)} %bitcast.32.ridge_ref), custom_call_target="tpu_custom_call" | custom-call | tf_op jit(solution)/shard_map/pallas_call | solution.py:29
  126.0 9.0 %all_to_all.78 = f32[8,1,256]{2,1,0:T(1,128)S(1)} all-to-all(f32[8,1,256]{2,1,0:T(1,128)S(1)} %copy.10), channel_id=1, replica_groups=mesh['row_0'=2,'row_1'=2,'row_2'=4,'col_0'=4,'col_1'=2] {'row_0','row_2'}, dimensions={0} | all-to-all | bytes 16384 | tf_op jit(solution)/shard_map/all_to_all | solution.py:42
  135.0 2.0 %collective-permute-start.15 = (f32[8,256]{1,0:T(8,128)S(1)}, f32[8,256]{1,0:T(8,128)S(1)}, u32[]{:S(2)}, u32[]{:S(2)}) collective-permute-start(f32[8,256]{1,0:T(8,128)S(1)} %bitcast.53), channel_id=1, source_target_pairs={{0,1},{1,0},{2,3},{3,2},{4,5},{5,4},{6,7},{7,6},{8,9},{9,8},{10,11... | collective-permute-start | bytes 24584 | tf_op jit(solution)/shard_map/ppermute | solution.py:379
  137.8 2.8 %shard_map.89 = f32[8,8,256]{2,1,0:T(8,128)S(1)} custom-call(f32[512,2048]{1,0:T(8,128)S(1)} %get-tuple-element.55.refs_0_, f32[512,2048]{1,0:T(8,128)S(1)} %get-tuple-element.58.refs_1_, f32[512,2048]{1,0:T(8,128)S(1)} %get-tuple-element.61.refs_2_, f32[512,2048]{1,0:T(8,128)S(1)} %get-tuple-element.64.refs_3_, f32[512,2048]{1,0:T(8,128)S(1)} %get-tuple-element.67.refs_4_, ...), custom_call_target="tpu_custom_call" | custom-call | tf_op jit(solution)/shard_map/pallas_call | solution.py:29
  140.6 7.7 %all_to_all.79.parts_ref = f32[8,8,256]{2,1,0:T(8,128)S(1)} all-to-all(f32[8,8,256]{2,1,0:T(8,128)S(1)} %shard_map.89), channel_id=1, replica_groups=mesh['row_0'=2,'row_1'=2,'row_2'=4,'col_0'=4,'col_1'=2] {'row_1','col_0'}, dimensions={0} | all-to-all | bytes 131072 | tf_op jit(solution)/shard_map/all_to_all | solution.py:42
  148.8 15.5 %all_to_all.80 = f32[128,1,384]{2,1,0:T(1,128)S(1)} all-to-all(f32[128,1,384]{2,1,0:T(1,128)S(1)} %copy.11), channel_id=1, replica_groups=mesh['row_0'=2,'row_1'=2,'row_2'=4,'col_0'=4,'col_1'=2] {'col_0','col_1'..., dimensions={0} | all-to-all | bytes 393216 | tf_op jit(solution)/shard_map/all_to_all | solution.py:42
  165.3 14.2 %all_to_all.81 = f32[128,1,256]{2,1,0:T(1,128)S(1)} all-to-all(f32[128,1,256]{2,1,0:T(1,128)S(1)} %copy.12), channel_id=1, replica_groups=mesh['row_0'=2,'row_1'=2,'row_2'=4,'col_0'=4,'col_1'=2] {'col_0','col_1'..., dimensions={0} | all-to-all | bytes 262144 | tf_op jit(solution)/shard_map/all_to_all | solution.py:42
  179.5 2.6 %shard_map.92 = f32[128,384]{1,0:T(8,128)S(1)} custom-call(f32[512,2048]{1,0:T(8,128)S(1)} %get-tuple-element.55.refs_0_, f32[512,2048]{1,0:T(8,128)S(1)} %get-tuple-element.58.refs_1_, f32[512,2048]{1,0:T(8,128)S(1)} %get-tuple-element.61.refs_2_, f32[512,2048]{1,0:T(8,128)S(1)} %get-tuple-element.64.refs_3_, f32[512,2048]{1,0:T(8,128)S(1)} %get-tuple-element.67.refs_4_, ...), custom_call_target="tpu_custom_call" | custom-call | tf_op jit(solution)/shard_map/pallas_call | solution.py:29
  182.3 14.6 %all_to_all.82 = f32[128,1,384]{2,1,0:T(1,128)S(1)} all-to-all(f32[128,1,384]{2,1,0:T(1,128)S(1)} %copy.13), channel_id=1, replica_groups=mesh['row_0'=2,'row_1'=2,'row_2'=4,'col_0'=4,'col_1'=2] {'col_0','col_1'..., dimensions={0} | all-to-all | bytes 393216 | tf_op jit(solution)/shard_map/all_to_all | solution.py:42
  (44 shorter events, 15.6 us)
Async XLA Ops:
  2.9 36.9 %all-to-all-start = ((bf16[8,256,384]{2,1,0:T(8,128)(2,1)}), bf16[8,256,384]{2,1,0:T(8,128)(2,1)S(1)}, u32[]{:S(2)}, u32[]{:S(2)}) async-start(bf16[8,256,384]{2,1,0:T(8,128)(2,1)} %get-tuple-element.50), calls=%async_computation | async-start | bytes 3145728 | tf_op jit(solution)/shard_map/all_to_all | solution.py:42
  11.4 21.8 %collective-permute-start = (bf16[256,128]{1,0:T(8,128)(2,1)S(1)}, bf16[256,128]{1,0:T(8,128)(2,1)S(1)}, u32[]{:S(2)}, u32[]{:S(2)}) collective-permute-start(bf16[256,128]{1,0:T(8,128)(2,1)S(1)} %get-tuple-element.62.refs_0_), channel_id=1, source_target_pairs={{0,32},{2,34},{4,36},{6,38},{32,0},{34,2},{36,4},{38,6},{1,33},{3,... | collective-permute-start | bytes 196616 | tf_op jit(solution)/shard_map/ppermute | solution.py:464
  11.8 23.9 %collective-permute-start.1 = (bf16[256,128]{1,0:T(8,128)(2,1)S(1)}, bf16[256,128]{1,0:T(8,128)(2,1)S(1)}, u32[]{:S(2)}, u32[]{:S(2)}) collective-permute-start(bf16[256,128]{1,0:T(8,128)(2,1)S(1)} %get-tuple-element.62.refs_0_), channel_id=1, source_target_pairs={{0,2},{2,4},{4,6},{6,0},{32,34},{34,36},{36,38},{38,32},{1,3},{3,5... | collective-permute-start | bytes 196616 | tf_op jit(solution)/shard_map/ppermute | solution.py:464
  13.0 24.0 %collective-permute-start.2 = (bf16[256,128]{1,0:T(8,128)(2,1)S(1)}, bf16[256,128]{1,0:T(8,128)(2,1)S(1)}, u32[]{:S(2)}, u32[]{:S(2)}) collective-permute-start(bf16[256,128]{1,0:T(8,128)(2,1)S(1)} %get-tuple-element.62.refs_0_), channel_id=1, source_target_pairs={{0,34},{2,36},{4,38},{6,32},{32,2},{34,4},{36,6},{38,0},{1,35},{3,... | collective-permute-start | bytes 196616 | tf_op jit(solution)/shard_map/ppermute | solution.py:464
  15.0 22.0 %collective-permute-start.3 = (bf16[256,128]{1,0:T(8,128)(2,1)S(1)}, bf16[256,128]{1,0:T(8,128)(2,1)S(1)}, u32[]{:S(2)}, u32[]{:S(2)}) collective-permute-start(bf16[256,128]{1,0:T(8,128)(2,1)S(1)} %get-tuple-element.62.refs_0_), channel_id=1, source_target_pairs={{0,4},{2,6},{4,0},{6,2},{32,36},{34,38},{36,32},{38,34},{1,5},{3,7... | collective-permute-start | bytes 196616 | tf_op jit(solution)/shard_map/ppermute | solution.py:464
  16.5 20.6 %collective-permute-start.4 = (bf16[256,128]{1,0:T(8,128)(2,1)S(1)}, bf16[256,128]{1,0:T(8,128)(2,1)S(1)}, u32[]{:S(2)}, u32[]{:S(2)}) collective-permute-start(bf16[256,128]{1,0:T(8,128)(2,1)S(1)} %get-tuple-element.62.refs_0_), channel_id=1, source_target_pairs={{0,36},{2,38},{4,32},{6,34},{32,4},{34,6},{36,0},{38,2},{1,37},{3,... | collective-permute-start | bytes 196616 | tf_op jit(solution)/shard_map/ppermute | solution.py:464
  33.2 3.8 %collective-permute-start.5 = (bf16[256,128]{1,0:T(8,128)(2,1)S(1)}, bf16[256,128]{1,0:T(8,128)(2,1)S(1)}, u32[]{:S(2)}, u32[]{:S(2)}) collective-permute-start(bf16[256,128]{1,0:T(8,128)(2,1)S(1)} %get-tuple-element.62.refs_0_), channel_id=1, source_target_pairs={{0,6},{2,0},{4,2},{6,4},{32,38},{34,32},{36,34},{38,36},{1,7},{3,1... | collective-permute-start | bytes 196616 | tf_op jit(solution)/shard_map/ppermute | solution.py:464
  35.7 4.1 %collective-permute-start.6 = (bf16[256,128]{1,0:T(8,128)(2,1)S(1)}, bf16[256,128]{1,0:T(8,128)(2,1)S(1)}, u32[]{:S(2)}, u32[]{:S(2)}) collective-permute-start(bf16[256,128]{1,0:T(8,128)(2,1)S(1)} %get-tuple-element.62.refs_0_), channel_id=1, source_target_pairs={{0,38},{2,32},{4,34},{6,36},{32,6},{34,0},{36,2},{38,4},{1,39},{3,... | collective-permute-start | bytes 196616 | tf_op jit(solution)/shard_map/ppermute | solution.py:464
  39.8 5.9 %collective-permute-start.7 = (bf16[2048,384]{1,0:T(8,128)(2,1)S(1)}, bf16[2048,384]{1,0:T(8,128)(2,1)S(1)}, u32[]{:S(2)}, u32[]{:S(2)}) collective-permute-start(bf16[2048,384]{1,0:T(8,128)(2,1)S(1)} %bitcast.36), channel_id=1, source_target_pairs={{0,1},{1,0},{2,3},{3,2},{4,5},{5,4},{6,7},{7,6},{8,9},{9,8},{10,11... | collective-permute-start | bytes 4718600 | tf_op jit(solution)/shard_map/ppermute | solution.py:471
  47.6 17.5 %collective-permute-start.8 = (f32[256,256]{1,0:T(8,128)S(1)}, f32[256,256]{1,0:T(8,128)S(1)}, u32[]{:S(2)}, u32[]{:S(2)}) collective-permute-start(f32[256,256]{1,0:T(8,128)S(1)} %get-tuple-element.77), channel_id=1, source_target_pairs={{0,36},{2,38},{4,32},{6,34},{32,4},{34,6},{36,0},{38,2},{1,37},{3,... | collective-permute-start | bytes 786440 | tf_op jit(solution)/shard_map/ppermute | solution.py:464
  49.0 16.2 %collective-permute-start.9 = (f32[256,256]{1,0:T(8,128)S(1)}, f32[256,256]{1,0:T(8,128)S(1)}, u32[]{:S(2)}, u32[]{:S(2)}) collective-permute-start(f32[256,256]{1,0:T(8,128)S(1)} %get-tuple-element.78), channel_id=1, source_target_pairs={{0,4},{2,6},{4,0},{6,2},{32,36},{34,38},{36,32},{38,34},{1,5},{3,7... | collective-permute-start | bytes 786440 | tf_op jit(solution)/shard_map/ppermute | solution.py:464
  54.9 25.3 %copy-start = (bf16[256,256]{1,0:T(8,128)(2,1)S(1)}, bf16[256,256]{1,0:T(8,128)(2,1)}, u32[]{:S(2)}) copy-start(bf16[256,256]{1,0:T(8,128)(2,1)} %refs_8_.1) | copy-start | bytes 393220
  54.9 25.3 %copy-start.1 = (f32[256]{0:T(256)S(1)}, f32[256]{0:T(256)}, u32[]{:S(2)}) copy-start(f32[256]{0:T(256)} %param.8) | copy-start | bytes 3076
  58.0 12.6 %collective-permute-start.10 = (f32[256,256]{1,0:T(8,128)S(1)}, f32[256,256]{1,0:T(8,128)S(1)}, u32[]{:S(2)}, u32[]{:S(2)}) collective-permute-start(f32[256,256]{1,0:T(8,128)S(1)} %get-tuple-element.79), channel_id=1, source_target_pairs={{0,38},{2,32},{4,34},{6,36},{32,6},{34,0},{36,2},{38,4},{1,39},{3,... | collective-permute-start | bytes 786440 | tf_op jit(solution)/shard_map/ppermute | solution.py:464
  60.0 15.6 %collective-permute-start.11 = (f32[256,256]{1,0:T(8,128)S(1)}, f32[256,256]{1,0:T(8,128)S(1)}, u32[]{:S(2)}, u32[]{:S(2)}) collective-permute-start(f32[256,256]{1,0:T(8,128)S(1)} %get-tuple-element.80), channel_id=1, source_target_pairs={{0,6},{2,0},{4,2},{6,4},{32,38},{34,32},{36,34},{38,36},{1,7},{3,1... | collective-permute-start | bytes 786440 | tf_op jit(solution)/shard_map/ppermute | solution.py:464
  61.4 14.2 %collective-permute-start.12 = (f32[256,256]{1,0:T(8,128)S(1)}, f32[256,256]{1,0:T(8,128)S(1)}, u32[]{:S(2)}, u32[]{:S(2)}) collective-permute-start(f32[256,256]{1,0:T(8,128)S(1)} %get-tuple-element.81), channel_id=1, source_target_pairs={{0,34},{2,36},{4,38},{6,32},{32,2},{34,4},{36,6},{38,0},{1,35},{3,... | collective-permute-start | bytes 786440 | tf_op jit(solution)/shard_map/ppermute | solution.py:464
  65.1 12.0 %collective-permute-start.13 = (f32[256,256]{1,0:T(8,128)S(1)}, f32[256,256]{1,0:T(8,128)S(1)}, u32[]{:S(2)}, u32[]{:S(2)}) collective-permute-start(f32[256,256]{1,0:T(8,128)S(1)} %get-tuple-element.82), channel_id=1, source_target_pairs={{0,2},{2,4},{4,6},{6,0},{32,34},{34,36},{36,38},{38,32},{1,3},{3,5... | collective-permute-start | bytes 786440 | tf_op jit(solution)/shard_map/ppermute | solution.py:464
  65.2 15.0 %collective-permute-start.14 = (f32[256,256]{1,0:T(8,128)S(1)}, f32[256,256]{1,0:T(8,128)S(1)}, u32[]{:S(2)}, u32[]{:S(2)}) collective-permute-start(f32[256,256]{1,0:T(8,128)S(1)} %get-tuple-element.83), channel_id=1, source_target_pairs={{0,32},{2,34},{4,36},{6,38},{32,0},{34,2},{36,4},{38,6},{1,33},{3,... | collective-permute-start | bytes 786440 | tf_op jit(solution)/shard_map/ppermute | solution.py:464
  135.0 2.8 %collective-permute-start.15 = (f32[8,256]{1,0:T(8,128)S(1)}, f32[8,256]{1,0:T(8,128)S(1)}, u32[]{:S(2)}, u32[]{:S(2)}) collective-permute-start(f32[8,256]{1,0:T(8,128)S(1)} %bitcast.53), channel_id=1, source_target_pairs={{0,1},{1,0},{2,3},{3,2},{4,5},{5,4},{6,7},{7,6},{8,9},{9,8},{10,11... | collective-permute-start | bytes 24584 | tf_op jit(solution)/shard_map/ppermute | solution.py:379

commit v5 on v3

--- a/solution.py
+++ b/solution.py
@@ -21,7 +21,7 @@
 BF16 = jnp.bfloat16
 HIGH = lax.Precision.HIGHEST
 KERN_SPACE = pltpu.VMEM
-ORDER = (2, 1, 3, 0)
+ORDER = (1, 3, 2, 0)
 KLIMIT = 4
 KLIMIT2 = 4
 
@@ -463,11 +463,14 @@
         ]
         return lax.ppermute(value, ROWS, pairs) if shift or flip else value
 
-    chunks = {
-        (shift, flip): along_rows(parts, shift, flip) for shift in ORDER for flip in (0, 1)
-    }
+    chunks = {}
+    for shift in ORDER:
+        for flip in (0, 1):
+            chunks[shift, flip] = along_rows(parts, shift, flip)
     message = exchanged(copies, NEAR_COLUMNS).reshape(-1, 128 + rank)
-    message, chunks = lax.optimization_barrier((message, chunks))
+    early = {key: value for key, value in chunks.items() if key[0] != 2}
+    message, early = lax.optimization_barrier((message, early))
+    chunks.update(early)
     partner = lax.ppermute(message, "col_1", [(0, 1), (1, 0)])
     norm = call(norms_body, shape(8, message.shape[0]), message)
     kerns, before, sums = {}, {}, []

time: 196 us -> 204 us (1.041)
  starting transfers between devices: 30.5 us -> 36.2 us
    ppermute x14, starting transfers between devices: 19.1 us -> 25.2 us  [along_rows(): return lax.ppermute(value, ROWS, pairs) if shift or flip else value]
  transfers between devices with their start and end apart: 16 -> 16, of which waited for: 7 -> 6; matrix products, arithmetic and copies ran while one was open for 0% -> 0% of each run, Pallas kernels for 6% -> 6%
where the time goes in v5:
time: 204 us; the launch traced here: 203 us
  blocking collectives  97.9 us (48%)
  starting transfers between devices  36.2 us (18%)
  waiting for transfers between devices  33.5 us (16%)
  Pallas kernels  32.9 us (16%)
    all_to_all x7, blocking collectives, exchanged(): return lax.all_to_all(pieces, axes, 0, 0, tiled=True)  97.9 us
    ppermute x14, waiting for transfers between devices, along_rows(): return lax.ppermute(value, ROWS, pairs) if shift or flip else value  31.8 us
    pallas_call x18, Pallas kernels, call(): pl.pallas_call(body, out_shape=outs, scratch_shapes=list(scratch), compil...  30.6 us
    ppermute x14, starting transfers between devices, along_rows(): return lax.ppermute(value, ROWS, pairs) if shift or flip else value  25.2 us
    all_to_all x1, starting transfers between devices, exchanged(): return lax.all_to_all(pieces, axes, 0, 0, tiled=True)  8.49 us
  transfers between devices with their start and end apart: 16, of which 6 were waited for; matrix products, arithmetic and copies ran while one was open for 0% of the time, Pallas kernels for 6%

profile of v5, /device:TPU:1, one launch (start us, length us, event | category | flops | bytes accessed | tf_op | source)
XLA Modules:
  0.0 203.3 jit_solution(10029659206003949467)
XLA Ops:
  0.6 2.3 %parts.1 = (bf16[256,128]{1,0:T(8,128)(2,1)S(1)}, bf16[8,256,384]{2,1,0:T(8,128)(2,1)}) custom-call(f32[64,256]{1,0:T(8,128)} %bitcast.60, f32[1,64]{1,0:T(1,128)} %bitcast.61, bf16[256,256]{1,0:T(8,128)(2,1)} %refs_8_.1), custom_call_target="tpu_custom_call" | custom-call | tf_op jit(solution)/shard_map/parts/pallas_call | solution.py:88
  2.9 8.5 %all-to-all-start = ((bf16[8,256,384]{2,1,0:T(8,128)(2,1)}), bf16[8,256,384]{2,1,0:T(8,128)(2,1)S(1)}, u32[]{:S(2)}, u32[]{:S(2)}) async-start(bf16[8,256,384]{2,1,0:T(8,128)(2,1)} %get-tuple-element.48), calls=%async_computation | async-start | bytes 3145728 | tf_op jit(solution)/shard_map/all_to_all | solution.py:43
  13.0 2.0 collective-permute-start.2
  15.0 1.5 collective-permute-start.3
  16.9 16.3 %collective-permute-done.refs_1_ = bf16[256,128]{1,0:T(8,128)(2,1)S(1)} collective-permute-done((bf16[256,128]{1,0:T(8,128)(2,1)S(1)}, bf16[256,128]{1,0:T(8,128)(2,1)S(1)}, u32[]{:S(2)}, u32[]{:S(2)}) %collective-permute-start) | collective-permute-done | bytes 65568 | tf_op jit(solution)/shard_map/ppermute | solution.py:464
  34.1 2.5 %collective-permute-start.7 = (bf16[2048,384]{1,0:T(8,128)(2,1)S(1)}, bf16[2048,384]{1,0:T(8,128)(2,1)S(1)}, u32[]{:S(2)}, u32[]{:S(2)}) collective-permute-start(bf16[2048,384]{1,0:T(8,128)(2,1)S(1)} %bitcast.36), channel_id=1, source_target_pairs={{0,1},{1,0},{2,3},{3,2},{4,5},{5,4},{6,7},{7,6},{8,9},{9,8},{10,11... | collective-permute-start | bytes 4718600 | tf_op jit(solution)/shard_map/ppermute | solution.py:474
  37.1 1.7 shard_map.77
  40.2 1.4 shard_map.82
  41.6 2.7 %collective-permute-start.8 = (f32[256,256]{1,0:T(8,128)S(1)}, f32[256,256]{1,0:T(8,128)S(1)}, u32[]{:S(2)}, u32[]{:S(2)}) collective-permute-start(f32[256,256]{1,0:T(8,128)S(1)} %get-tuple-element.73), channel_id=1, source_target_pairs={{0,38},{2,32},{4,34},{6,36},{32,6},{34,0},{36,2},{38,4},{1,39},{3,... | collective-permute-start | bytes 786440 | tf_op jit(solution)/shard_map/ppermute | solution.py:464
  45.0 3.5 %collective-permute-start.6 = (bf16[256,128]{1,0:T(8,128)(2,1)S(1)}, bf16[256,128]{1,0:T(8,128)(2,1)S(1)}, u32[]{:S(2)}, u32[]{:S(2)}) collective-permute-start(bf16[256,128]{1,0:T(8,128)(2,1)S(1)} %get-tuple-element.58.refs_0_), channel_id=1, source_target_pairs={{0,36},{2,38},{4,32},{6,34},{32,4},{34,6},{36,0},{38,2},{1,37},{3,... | collective-permute-start | bytes 196616 | tf_op jit(solution)/shard_map/ppermute | solution.py:464
  48.5 1.7 shard_map.78
  50.2 1.7 shard_map.80
  52.0 1.7 shard_map.79
  53.7 1.4 shard_map.83
  55.1 8.5 %collective-permute-start.10 = (f32[256,256]{1,0:T(8,128)S(1)}, f32[256,256]{1,0:T(8,128)S(1)}, u32[]{:S(2)}, u32[]{:S(2)}) collective-permute-start(f32[256,256]{1,0:T(8,128)S(1)} %get-tuple-element.75), channel_id=1, source_target_pairs={{0,34},{2,36},{4,38},{6,32},{32,2},{34,4},{36,6},{38,0},{1,35},{3,... | collective-permute-start | bytes 786440 | tf_op jit(solution)/shard_map/ppermute | solution.py:464
  63.6 1.4 shard_map.84
  65.0 2.4 %collective-permute-start.12 = (f32[256,256]{1,0:T(8,128)S(1)}, f32[256,256]{1,0:T(8,128)S(1)}, u32[]{:S(2)}, u32[]{:S(2)}) collective-permute-start(f32[256,256]{1,0:T(8,128)S(1)} %get-tuple-element.77), channel_id=1, source_target_pairs={{0,36},{2,38},{4,32},{6,34},{32,4},{34,6},{36,0},{38,2},{1,37},{3,... | collective-permute-start | bytes 786440 | tf_op jit(solution)/shard_map/ppermute | solution.py:464
  67.4 1.4 shard_map.85
  68.9 1.5 collective-permute-start.13
  71.4 3.2 %collective-permute-done.11.refs_3_ = f32[256,256]{1,0:T(8,128)S(1)} collective-permute-done((f32[256,256]{1,0:T(8,128)S(1)}, f32[256,256]{1,0:T(8,128)S(1)}, u32[]{:S(2)}, u32[]{:S(2)}) %collective-permute-start.11) | collective-permute-done | bytes 262176 | tf_op jit(solution)/shard_map/ppermute | solution.py:464
  74.6 7.4 %collective-permute-done.12.refs_4_ = f32[256,256]{1,0:T(8,128)S(1)} collective-permute-done((f32[256,256]{1,0:T(8,128)S(1)}, f32[256,256]{1,0:T(8,128)S(1)}, u32[]{:S(2)}, u32[]{:S(2)}) %collective-permute-start.12) | collective-permute-done | bytes 262176 | tf_op jit(solution)/shard_map/ppermute | solution.py:464
  82.1 4.8 %collective-permute-done.13.refs_5_ = f32[256,256]{1,0:T(8,128)S(1)} collective-permute-done((f32[256,256]{1,0:T(8,128)S(1)}, f32[256,256]{1,0:T(8,128)S(1)}, u32[]{:S(2)}, u32[]{:S(2)}) %collective-permute-start.13) | collective-permute-done | bytes 262176 | tf_op jit(solution)/shard_map/ppermute | solution.py:464
  88.1 20.0 %all_to_all.76 = f32[128,1,512]{2,1,0:T(1,128)S(1)} all-to-all(f32[128,1,512]{2,1,0:T(1,128)S(1)} %copy.8), channel_id=1, replica_groups=mesh['row_0'=2,'row_1'=2,'row_2'=4,'col_0'=4,'col_1'=2] {'col_0','col_1'..., dimensions={0} | all-to-all | bytes 524288 | tf_op jit(solution)/shard_map/all_to_all | solution.py:43
  108.5 15.2 %all_to_all.77 = f32[128,1,512]{2,1,0:T(1,128)S(1)} all-to-all(f32[128,1,512]{2,1,0:T(1,128)S(1)} %copy.9), channel_id=1, replica_groups=mesh['row_0'=2,'row_1'=2,'row_2'=4,'col_0'=4,'col_1'=2] {'col_0','col_1'..., dimensions={0} | all-to-all | bytes 524288 | tf_op jit(solution)/shard_map/all_to_all | solution.py:43
  123.7 9.5 %shard_map.88 = (f32[256,256]{1,0:T(8,128)S(1)}, f32[8,256]{1,0:T(8,128)S(1)}, f32[16,256]{1,0:T(8,128)S(1)}) custom-call(f32[128,512]{1,0:T(8,128)S(1)} %bitcast.44, f32[256,256]{1,0:T(8,128)S(1)} %get-tuple-element.82.sketch_ref, f32[1,256]{1,0:T(1,128)S(1)} %bitcast.55, f32[1,1]{1,0:T(1,128)} %bitcast.32.ridge_ref), custom_call_target="tpu_custom_call" | custom-call | tf_op jit(solution)/shard_map/pallas_call | solution.py:30
  133.3 10.6 %all_to_all.78 = f32[16,1,256]{2,1,0:T(1,128)S(1)} all-to-all(f32[16,1,256]{2,1,0:T(1,128)S(1)} %copy.10), channel_id=1, replica_groups=mesh['row_0'=2,'row_1'=2,'row_2'=4,'col_0'=4,'col_1'=2] {'col_1','row_0'..., dimensions={0} | all-to-all | bytes 32768 | tf_op jit(solution)/shard_map/all_to_all | solution.py:43
  143.9 2.4 %shard_map.89 = f32[8,8,256]{2,1,0:T(8,128)S(1)} custom-call(f32[512,2048]{1,0:T(8,128)S(1)} %get-tuple-element.53.refs_0_, f32[512,2048]{1,0:T(8,128)S(1)} %get-tuple-element.56.refs_1_, f32[512,2048]{1,0:T(8,128)S(1)} %get-tuple-element.57.refs_2_, f32[512,2048]{1,0:T(8,128)S(1)} %get-tuple-element.60.refs_3_, f32[512,2048]{1,0:T(8,128)S(1)} %get-tuple-element.63.refs_4_, ...), custom_call_target="tpu_custom_call" | custom-call | tf_op jit(solution)/shard_map/pallas_call | solution.py:30
  146.3 7.7 %all_to_all.79.parts_ref = f32[8,8,256]{2,1,0:T(8,128)S(1)} all-to-all(f32[8,8,256]{2,1,0:T(8,128)S(1)} %shard_map.89), channel_id=1, replica_groups=mesh['row_0'=2,'row_1'=2,'row_2'=4,'col_0'=4,'col_1'=2] {'row_1','col_0'}, dimensions={0} | all-to-all | bytes 131072 | tf_op jit(solution)/shard_map/all_to_all | solution.py:43
  154.5 15.6 %all_to_all.80 = f32[128,1,384]{2,1,0:T(1,128)S(1)} all-to-all(f32[128,1,384]{2,1,0:T(1,128)S(1)} %copy.11), channel_id=1, replica_groups=mesh['row_0'=2,'row_1'=2,'row_2'=4,'col_0'=4,'col_1'=2] {'col_0','col_1'..., dimensions={0} | all-to-all | bytes 393216 | tf_op jit(solution)/shard_map/all_to_all | solution.py:43
  171.0 14.2 %all_to_all.81 = f32[128,1,256]{2,1,0:T(1,128)S(1)} all-to-all(f32[128,1,256]{2,1,0:T(1,128)S(1)} %copy.12), channel_id=1, replica_groups=mesh['row_0'=2,'row_1'=2,'row_2'=4,'col_0'=4,'col_1'=2] {'col_0','col_1'..., dimensions={0} | all-to-all | bytes 262144 | tf_op jit(solution)/shard_map/all_to_all | solution.py:43
  185.3 2.6 %shard_map.92 = f32[128,384]{1,0:T(8,128)S(1)} custom-call(f32[512,2048]{1,0:T(8,128)S(1)} %get-tuple-element.53.refs_0_, f32[512,2048]{1,0:T(8,128)S(1)} %get-tuple-element.56.refs_1_, f32[512,2048]{1,0:T(8,128)S(1)} %get-tuple-element.57.refs_2_, f32[512,2048]{1,0:T(8,128)S(1)} %get-tuple-element.60.refs_3_, f32[512,2048]{1,0:T(8,128)S(1)} %get-tuple-element.63.refs_4_, ...), custom_call_target="tpu_custom_call" | custom-call | tf_op jit(solution)/shard_map/pallas_call | solution.py:30
  188.1 14.6 %all_to_all.82 = f32[128,1,384]{2,1,0:T(1,128)S(1)} all-to-all(f32[128,1,384]{2,1,0:T(1,128)S(1)} %copy.13), channel_id=1, replica_groups=mesh['row_0'=2,'row_1'=2,'row_2'=4,'col_0'=4,'col_1'=2] {'col_0','col_1'..., dimensions={0} | all-to-all | bytes 393216 | tf_op jit(solution)/shard_map/all_to_all | solution.py:43
  (42 shorter events, 9.8 us)
Async XLA Ops:
  2.9 31.2 %all-to-all-start = ((bf16[8,256,384]{2,1,0:T(8,128)(2,1)}), bf16[8,256,384]{2,1,0:T(8,128)(2,1)S(1)}, u32[]{:S(2)}, u32[]{:S(2)}) async-start(bf16[8,256,384]{2,1,0:T(8,128)(2,1)} %get-tuple-element.48), calls=%async_computation | async-start | bytes 3145728 | tf_op jit(solution)/shard_map/all_to_all | solution.py:43
  11.4 21.8 %collective-permute-start = (bf16[256,128]{1,0:T(8,128)(2,1)S(1)}, bf16[256,128]{1,0:T(8,128)(2,1)S(1)}, u32[]{:S(2)}, u32[]{:S(2)}) collective-permute-start(bf16[256,128]{1,0:T(8,128)(2,1)S(1)} %get-tuple-element.58.refs_0_), channel_id=1, source_target_pairs={{0,32},{2,34},{4,36},{6,38},{32,0},{34,2},{36,4},{38,6},{1,33},{3,... | collective-permute-start | bytes 196616 | tf_op jit(solution)/shard_map/ppermute | solution.py:464
  11.8 21.4 %collective-permute-start.1 = (bf16[256,128]{1,0:T(8,128)(2,1)S(1)}, bf16[256,128]{1,0:T(8,128)(2,1)S(1)}, u32[]{:S(2)}, u32[]{:S(2)}) collective-permute-start(bf16[256,128]{1,0:T(8,128)(2,1)S(1)} %get-tuple-element.58.refs_0_), channel_id=1, source_target_pairs={{0,2},{2,4},{4,6},{6,0},{32,34},{34,36},{36,38},{38,32},{1,3},{3,5... | collective-permute-start | bytes 196616 | tf_op jit(solution)/shard_map/ppermute | solution.py:464
  13.0 20.2 %collective-permute-start.2 = (bf16[256,128]{1,0:T(8,128)(2,1)S(1)}, bf16[256,128]{1,0:T(8,128)(2,1)S(1)}, u32[]{:S(2)}, u32[]{:S(2)}) collective-permute-start(bf16[256,128]{1,0:T(8,128)(2,1)S(1)} %get-tuple-element.58.refs_0_), channel_id=1, source_target_pairs={{0,34},{2,36},{4,38},{6,32},{32,2},{34,4},{36,6},{38,0},{1,35},{3,... | collective-permute-start | bytes 196616 | tf_op jit(solution)/shard_map/ppermute | solution.py:464
  15.0 18.2 %collective-permute-start.3 = (bf16[256,128]{1,0:T(8,128)(2,1)S(1)}, bf16[256,128]{1,0:T(8,128)(2,1)S(1)}, u32[]{:S(2)}, u32[]{:S(2)}) collective-permute-start(bf16[256,128]{1,0:T(8,128)(2,1)S(1)} %get-tuple-element.58.refs_0_), channel_id=1, source_target_pairs={{0,6},{2,0},{4,2},{6,4},{32,38},{34,32},{36,34},{38,36},{1,7},{3,1... | collective-permute-start | bytes 196616 | tf_op jit(solution)/shard_map/ppermute | solution.py:464
  16.5 16.7 %collective-permute-start.4 = (bf16[256,128]{1,0:T(8,128)(2,1)S(1)}, bf16[256,128]{1,0:T(8,128)(2,1)S(1)}, u32[]{:S(2)}, u32[]{:S(2)}) collective-permute-start(bf16[256,128]{1,0:T(8,128)(2,1)S(1)} %get-tuple-element.58.refs_0_), channel_id=1, source_target_pairs={{0,38},{2,32},{4,34},{6,36},{32,6},{34,0},{36,2},{38,4},{1,39},{3,... | collective-permute-start | bytes 196616 | tf_op jit(solution)/shard_map/ppermute | solution.py:464
  34.1 5.5 %collective-permute-start.7 = (bf16[2048,384]{1,0:T(8,128)(2,1)S(1)}, bf16[2048,384]{1,0:T(8,128)(2,1)S(1)}, u32[]{:S(2)}, u32[]{:S(2)}) collective-permute-start(bf16[2048,384]{1,0:T(8,128)(2,1)S(1)} %bitcast.36), channel_id=1, source_target_pairs={{0,1},{1,0},{2,3},{3,2},{4,5},{5,4},{6,7},{7,6},{8,9},{9,8},{10,11... | collective-permute-start | bytes 4718600 | tf_op jit(solution)/shard_map/ppermute | solution.py:474
  41.6 27.3 %collective-permute-start.8 = (f32[256,256]{1,0:T(8,128)S(1)}, f32[256,256]{1,0:T(8,128)S(1)}, u32[]{:S(2)}, u32[]{:S(2)}) collective-permute-start(f32[256,256]{1,0:T(8,128)S(1)} %get-tuple-element.73), channel_id=1, source_target_pairs={{0,38},{2,32},{4,34},{6,36},{32,6},{34,0},{36,2},{38,4},{1,39},{3,... | collective-permute-start | bytes 786440 | tf_op jit(solution)/shard_map/ppermute | solution.py:464
  44.3 26.1 %collective-permute-start.9 = (f32[256,256]{1,0:T(8,128)S(1)}, f32[256,256]{1,0:T(8,128)S(1)}, u32[]{:S(2)}, u32[]{:S(2)}) collective-permute-start(f32[256,256]{1,0:T(8,128)S(1)} %get-tuple-element.74), channel_id=1, source_target_pairs={{0,6},{2,0},{4,2},{6,4},{32,38},{34,32},{36,34},{38,36},{1,7},{3,1... | collective-permute-start | bytes 786440 | tf_op jit(solution)/shard_map/ppermute | solution.py:464
  44.8 7.2 %collective-permute-start.5 = (bf16[256,128]{1,0:T(8,128)(2,1)S(1)}, bf16[256,128]{1,0:T(8,128)(2,1)S(1)}, u32[]{:S(2)}, u32[]{:S(2)}) collective-permute-start(bf16[256,128]{1,0:T(8,128)(2,1)S(1)} %get-tuple-element.58.refs_0_), channel_id=1, source_target_pairs={{0,4},{2,6},{4,0},{6,2},{32,36},{34,38},{36,32},{38,34},{1,5},{3,7... | collective-permute-start | bytes 196616 | tf_op jit(solution)/shard_map/ppermute | solution.py:464
  45.0 7.0 %collective-permute-start.6 = (bf16[256,128]{1,0:T(8,128)(2,1)S(1)}, bf16[256,128]{1,0:T(8,128)(2,1)S(1)}, u32[]{:S(2)}, u32[]{:S(2)}) collective-permute-start(bf16[256,128]{1,0:T(8,128)(2,1)S(1)} %get-tuple-element.58.refs_0_), channel_id=1, source_target_pairs={{0,36},{2,38},{4,32},{6,34},{32,4},{34,6},{36,0},{38,2},{1,37},{3,... | collective-permute-start | bytes 196616 | tf_op jit(solution)/shard_map/ppermute | solution.py:464
  51.9 34.9 %copy-start = (bf16[256,256]{1,0:T(8,128)(2,1)S(1)}, bf16[256,256]{1,0:T(8,128)(2,1)}, u32[]{:S(2)}) copy-start(bf16[256,256]{1,0:T(8,128)(2,1)} %refs_8_.1) | copy-start | bytes 393220
  52.0 34.9 %copy-start.1 = (f32[256]{0:T(256)S(1)}, f32[256]{0:T(256)}, u32[]{:S(2)}) copy-start(f32[256]{0:T(256)} %param.8) | copy-start | bytes 3076
  55.1 16.3 %collective-permute-start.10 = (f32[256,256]{1,0:T(8,128)S(1)}, f32[256,256]{1,0:T(8,128)S(1)}, u32[]{:S(2)}, u32[]{:S(2)}) collective-permute-start(f32[256,256]{1,0:T(8,128)S(1)} %get-tuple-element.75), channel_id=1, source_target_pairs={{0,34},{2,36},{4,38},{6,32},{32,2},{34,4},{36,6},{38,0},{1,35},{3,... | collective-permute-start | bytes 786440 | tf_op jit(solution)/shard_map/ppermute | solution.py:464
  63.6 11.0 %collective-permute-start.11 = (f32[256,256]{1,0:T(8,128)S(1)}, f32[256,256]{1,0:T(8,128)S(1)}, u32[]{:S(2)}, u32[]{:S(2)}) collective-permute-start(f32[256,256]{1,0:T(8,128)S(1)} %get-tuple-element.76), channel_id=1, source_target_pairs={{0,2},{2,4},{4,6},{6,0},{32,34},{34,36},{36,38},{38,32},{1,3},{3,5... | collective-permute-start | bytes 786440 | tf_op jit(solution)/shard_map/ppermute | solution.py:464
  65.0 17.0 %collective-permute-start.12 = (f32[256,256]{1,0:T(8,128)S(1)}, f32[256,256]{1,0:T(8,128)S(1)}, u32[]{:S(2)}, u32[]{:S(2)}) collective-permute-start(f32[256,256]{1,0:T(8,128)S(1)} %get-tuple-element.77), channel_id=1, source_target_pairs={{0,36},{2,38},{4,32},{6,34},{32,4},{34,6},{36,0},{38,2},{1,37},{3,... | collective-permute-start | bytes 786440 | tf_op jit(solution)/shard_map/ppermute | solution.py:464
  68.9 18.0 %collective-permute-start.13 = (f32[256,256]{1,0:T(8,128)S(1)}, f32[256,256]{1,0:T(8,128)S(1)}, u32[]{:S(2)}, u32[]{:S(2)}) collective-permute-start(f32[256,256]{1,0:T(8,128)S(1)} %get-tuple-element.78), channel_id=1, source_target_pairs={{0,4},{2,6},{4,0},{6,2},{32,36},{34,38},{36,32},{38,34},{1,5},{3,7... | collective-permute-start | bytes 786440 | tf_op jit(solution)/shard_map/ppermute | solution.py:464
  70.3 16.6 %collective-permute-start.14 = (f32[256,256]{1,0:T(8,128)S(1)}, f32[256,256]{1,0:T(8,128)S(1)}, u32[]{:S(2)}, u32[]{:S(2)}) collective-permute-start(f32[256,256]{1,0:T(8,128)S(1)} %get-tuple-element.79), channel_id=1, source_target_pairs={{0,32},{2,34},{4,36},{6,38},{32,0},{34,2},{36,4},{38,6},{1,33},{3,... | collective-permute-start | bytes 786440 | tf_op jit(solution)/shard_map/ppermute | solution.py:464
